TPU v7x, 64 devices: a 2x2x8 block of a 4x4x8 slice. The times are simulated.
64 devices in a mesh: dp: 4 (over x, y), tp: 16 (over z, core).
Axes of the slice: x: 2, y: 2, z: 8, core: 2. Of those that a mesh axis runs over, the one named last changes fastest.
The devices are a block of a 4x4x8 slice.
Arguments:
- x_in: bfloat16 [4, 1024, 2048], P('dp', 'tp'), parts along dimension 0
- y_grad: bfloat16 [4, 1024, 2048], P('dp', 'tp'), parts along dimension 0
- ln_par: float32 [2, 4, 2048], replicated
- bias_d: float32 [2, 2, 2048], replicated
- w_qkv: bfloat16 [2, 2048, 3, 16, 128], P(None, None, None, 'tp')
- w_out: bfloat16 [2, 16, 128, 2048], P(None, 'tp')
- w_up: bfloat16 [2, 2048, 8192], P(None, None, 'tp')
- b_up: float32 [2, 8192], P(None, 'tp')
- w_down: bfloat16 [2, 8192, 2048], P(None, 'tp')
Outputs:
- output 1: bfloat16 [4, 1024, 2048], P('dp', 'tp'), parts along dimension 0
- output 2: bfloat16 [4, 1024, 2048], P('dp', 'tp'), parts along dimension 0
- output 3: float32 [8, 4, 2048], P('dp'), parts along dimension 0
- output 4: float32 [8, 2, 2048], P('dp'), parts along dimension 0
- output 5: bfloat16 [8, 2048, 3, 16, 128], P('dp', None, None, 'tp'), parts along dimension 0
- output 6: bfloat16 [8, 16, 128, 2048], P('dp', 'tp'), parts along dimension 0
- output 7: bfloat16 [8, 2048, 8192], P('dp', None, 'tp'), parts along dimension 0
- output 8: float32 [8, 8192], P('dp', 'tp'), parts along dimension 0
- output 9: bfloat16 [8, 8192, 2048], P('dp', 'tp'), parts along dimension 0
There are 4 independent parts. A program takes and returns all parts, laid end to end along the dimension named above; an argument that names none is the same for every part.
All inputs are finite; a program needn't handle non-finite values.
Results may differ from a plain program's by a relative error of at most 0.02.
Values are sent between devices in bfloat16 or wider.
A program may use at most 768 MiB of HBM per device.

v0:
```python
import jax
import jax.numpy as jnp
from jax import lax
from jax.sharding import PartitionSpec as P


def layer_norm(row_vals, ln_gain, ln_shift):
    mean_val = jnp.mean(row_vals, axis=-1, keepdims=True)
    centered = row_vals - mean_val
    var_val = jnp.mean(centered * centered, axis=-1, keepdims=True)
    return centered * lax.rsqrt(var_val + 1e-5) * ln_gain + ln_shift


def gelu_tanh(pre_act):
    return jax.nn.gelu(pre_act, approximate=True)


def gather_rows(local_vals):
    return lax.all_gather(local_vals, 'tp', axis=1, tiled=True)


def scatter_rows(partial_vals, group_size):
    n_batch, seq_len, width = partial_vals.shape
    sent = partial_vals.astype(jnp.bfloat16).reshape(n_batch, group_size, seq_len // group_size, width)
    received = lax.all_to_all(sent, 'tp', 1, 1, tiled=True)
    return jnp.sum(received, axis=1, dtype=jnp.float32)


def causal_attention(q_vals, k_vals, v_vals):
    seq_len = q_vals.shape[1]
    score_scale = q_vals.shape[-1] ** -0.5
    scores = jnp.einsum('bqhe,bkhe->bhqk', q_vals, k_vals, preferred_element_type=jnp.float32) * score_scale
    positions = jnp.arange(seq_len)
    causal = positions[:, None] >= positions[None, :]
    scores = jnp.where(causal, scores, -1e30)
    prob_bf = jax.nn.softmax(scores, axis=-1).astype(jnp.bfloat16)
    attn_vals = jnp.einsum('bhqk,bkhe->bqhe', prob_bf, v_vals, preferred_element_type=jnp.float32).astype(jnp.bfloat16)
    return attn_vals, prob_bf


def attention_backward(d_attn, q_vals, k_vals, v_vals, prob_bf):
    score_scale = q_vals.shape[-1] ** -0.5
    d_prob = jnp.einsum('bqhe,bkhe->bhqk', d_attn, v_vals, preferred_element_type=jnp.float32)
    d_v = jnp.einsum('bhqk,bqhe->bkhe', prob_bf, d_attn, preferred_element_type=jnp.float32)
    row_dot = jnp.sum(d_prob * prob_bf, axis=-1, keepdims=True)
    d_score = (prob_bf * (d_prob - row_dot) * score_scale).astype(jnp.bfloat16)
    d_q = jnp.einsum('bhqk,bkhe->bqhe', d_score, k_vals, preferred_element_type=jnp.float32)
    d_k = jnp.einsum('bhqk,bqhe->bkhe', d_score, q_vals, preferred_element_type=jnp.float32)
    return d_q, d_k, d_v


def solution(mesh):
    group_size = mesh.shape['tp']

    def device_step(x_loc, dy_loc, ln_par, bias_d, w_qkv, w_out, w_up, b_up, w_down):
        n_layers = ln_par.shape[0]
        residual = x_loc.astype(jnp.float32)
        saved = []
        for layer_idx in range(n_layers):
            ln_vals = ln_par[layer_idx]
            bias_vals = bias_d[layer_idx]
            w_proj = w_qkv[layer_idx]
            res_one = residual
            h_all = gather_rows(layer_norm(res_one, ln_vals[0], ln_vals[1]).astype(jnp.bfloat16))
            q_vals = jnp.einsum('bsd,dhe->bshe', h_all, w_proj[:, 0], preferred_element_type=jnp.float32).astype(jnp.bfloat16)
            k_vals = jnp.einsum('bsd,dhe->bshe', h_all, w_proj[:, 1], preferred_element_type=jnp.float32).astype(jnp.bfloat16)
            v_vals = jnp.einsum('bsd,dhe->bshe', h_all, w_proj[:, 2], preferred_element_type=jnp.float32).astype(jnp.bfloat16)
            attn_vals, prob_bf = causal_attention(q_vals, k_vals, v_vals)
            attn_part = jnp.einsum('bshe,hed->bsd', attn_vals, w_out[layer_idx], preferred_element_type=jnp.float32)
            res_two = res_one + scatter_rows(attn_part, group_size) + bias_vals[0]
            h2_all = gather_rows(layer_norm(res_two, ln_vals[2], ln_vals[3]).astype(jnp.bfloat16))
            pre_act = jnp.einsum('bsd,df->bsf', h2_all, w_up[layer_idx], preferred_element_type=jnp.float32) + b_up[layer_idx]
            act_f, gelu_pull = jax.vjp(gelu_tanh, pre_act)
            act_vals = act_f.astype(jnp.bfloat16)
            mlp_part = jnp.einsum('bsf,fd->bsd', act_vals, w_down[layer_idx], preferred_element_type=jnp.float32)
            residual = res_two + scatter_rows(mlp_part, group_size) + bias_vals[1]
            saved.append((res_one, h_all, q_vals, k_vals, v_vals, prob_bf, attn_vals, res_two, h2_all, gelu_pull, act_vals))
        y_loc = residual.astype(jnp.bfloat16)

        d_res = dy_loc.astype(jnp.float32)
        layer_grads = [None] * n_layers
        for layer_idx in reversed(range(n_layers)):
            res_one, h_all, q_vals, k_vals, v_vals, prob_bf, attn_vals, res_two, h2_all, gelu_pull, act_vals = saved[layer_idx]
            ln_vals = ln_par[layer_idx]
            w_proj = w_qkv[layer_idx]
            d_bias_two = jnp.sum(d_res, axis=(0, 1))
            d_mlp_all = gather_rows(d_res.astype(jnp.bfloat16))
            d_wdown = jnp.einsum('bsf,bsd->fd', act_vals, d_mlp_all, preferred_element_type=jnp.float32)
            d_act = jnp.einsum('bsd,fd->bsf', d_mlp_all, w_down[layer_idx], preferred_element_type=jnp.float32)
            d_pre = gelu_pull(d_act)[0]
            d_bup = jnp.sum(d_pre, axis=(0, 1))
            d_pre_bf = d_pre.astype(jnp.bfloat16)
            d_wup = jnp.einsum('bsd,bsf->df', h2_all, d_pre_bf, preferred_element_type=jnp.float32)
            d_h2 = scatter_rows(jnp.einsum('bsf,df->bsd', d_pre_bf, w_up[layer_idx], preferred_element_type=jnp.float32), group_size)
            ln_pull = jax.vjp(layer_norm, res_two, ln_vals[2], ln_vals[3])[1]
            d_mid, d_gain_two, d_shift_two = ln_pull(d_h2)
            d_res = d_res + d_mid
            d_bias_one = jnp.sum(d_res, axis=(0, 1))
            d_attn_all = gather_rows(d_res.astype(jnp.bfloat16))
            d_wout = jnp.einsum('bshe,bsd->hed', attn_vals, d_attn_all, preferred_element_type=jnp.float32)
            d_attn = jnp.einsum('bsd,hed->bshe', d_attn_all, w_out[layer_idx], preferred_element_type=jnp.float32).astype(jnp.bfloat16)
            d_q, d_k, d_v = attention_backward(d_attn, q_vals, k_vals, v_vals, prob_bf)
            d_proj = [d_q.astype(jnp.bfloat16), d_k.astype(jnp.bfloat16), d_v.astype(jnp.bfloat16)]
            d_wqkv = jnp.stack([jnp.einsum('bsd,bshe->dhe', h_all, d_part, preferred_element_type=jnp.float32) for d_part in d_proj], axis=1)
            d_h_part = (jnp.einsum('bshe,dhe->bsd', d_proj[0], w_proj[:, 0], preferred_element_type=jnp.float32)
                        + jnp.einsum('bshe,dhe->bsd', d_proj[1], w_proj[:, 1], preferred_element_type=jnp.float32)
                        + jnp.einsum('bshe,dhe->bsd', d_proj[2], w_proj[:, 2], preferred_element_type=jnp.float32))
            d_h = scatter_rows(d_h_part, group_size)
            ln_pull = jax.vjp(layer_norm, res_one, ln_vals[0], ln_vals[1])[1]
            d_in, d_gain_one, d_shift_one = ln_pull(d_h)
            d_res = d_res + d_in
            layer_grads[layer_idx] = (jnp.stack([d_gain_one, d_shift_one, d_gain_two, d_shift_two]), jnp.stack([d_bias_one, d_bias_two]), d_wqkv, d_wout, d_wup, d_bup, d_wdown)
        small_grads = lax.psum((jnp.stack([grad_set[0] for grad_set in layer_grads]), jnp.stack([grad_set[1] for grad_set in layer_grads])), 'tp')
        return (y_loc, d_res.astype(jnp.bfloat16), small_grads[0], small_grads[1],
                jnp.stack([grad_set[2] for grad_set in layer_grads]).astype(jnp.bfloat16),
                jnp.stack([grad_set[3] for grad_set in layer_grads]).astype(jnp.bfloat16),
                jnp.stack([grad_set[4] for grad_set in layer_grads]).astype(jnp.bfloat16),
                jnp.stack([grad_set[5] for grad_set in layer_grads]),
                jnp.stack([grad_set[6] for grad_set in layer_grads]).astype(jnp.bfloat16))

    in_specs = (P('dp', 'tp', None), P('dp', 'tp', None), P(None, None, None), P(None, None, None),
                P(None, None, None, 'tp', None), P(None, 'tp', None, None), P(None, None, 'tp'), P(None, 'tp'), P(None, 'tp', None))
    out_specs = (P('dp', 'tp', None), P('dp', 'tp', None), P('dp', None, None), P('dp', None, None),
                 P('dp', None, None, 'tp', None), P('dp', 'tp', None, None), P('dp', None, 'tp'), P('dp', 'tp'), P('dp', 'tp', None))
    return jax.shard_map(device_step, mesh=mesh, in_specs=in_specs, out_specs=out_specs, check_vma=False)
```

profile of v0, /device:TPU:21, one launch (start us, length us, event | category | flops | bytes accessed | tf_op | source)
XLA Modules:
  0.0 1385.3 jit_solution(2021216544933458056)
XLA Ops:
  11.1 1.8 fusion.205
  13.0 3.2 slice_bitcast_fusion
  16.2 40.6 %all-gather.9.cloned.1.call-done = bf16[1,1024,2048]{2,1,0:T(8,128)(2,1)} async-done(((bf16[1,64,2048]{2,1,0:T(8,128)(2,1)}), bf16[1,1024,2048]{2,1,0:T(8,128)(2,1)}) %all-gather.9.cloned.1.call-update) | async-done | bytes 4194320 | tf_op jit(solution)/shard_map/all_gather | solution.py:19
  56.9 3.6 fusion.172
  64.4 2.4 fusion.166
  67.3 3.3 convolution_convert_fusion.5
  70.6 4.8 all-to-all-start
  75.6 93.0 %all-to-all-done = bf16[1,16,64,2048]{3,2,0,1:T(8,128)(2,1)} async-done(((bf16[1,16,64,2048]{3,2,0,1:T(8,128)(2,1)}), bf16[1,16,64,2048]{3,2,0,1:T(8,128)(2,1)}, u32[]{:S(2)}, u32[]{:S(2)}) %all-to-all-start) | async-done | bytes 4194336 | tf_op jit(solution)/shard_map/all_to_all | solution.py:25
  168.6 3.0 convert_reduce_fusion.11
  173.5 39.7 %all-gather.11.cloned.1.call-done = bf16[1,1024,2048]{2,1,0:T(8,128)(2,1)} async-done(((bf16[1,64,2048]{2,1,0:T(8,128)(2,1)}), bf16[1,1024,2048]{2,1,0:T(8,128)(2,1)}) %all-gather.11.cloned.1.call-update) | async-done | bytes 4194320 | tf_op jit(solution)/shard_map/all_gather | solution.py:19
  213.2 5.3 fusion.40
  218.5 2.6 convolution_convert_fusion.3
  221.2 99.8 %all_to_all.40 = bf16[1,16,64,2048]{3,2,0,1:T(8,128)(2,1)S(1)} all-to-all(bf16[1,16,64,2048]{3,2,0,1:T(8,128)(2,1)S(1)} %bitcast.442), channel_id=1, replica_groups=mesh['dp'=4,'tp'=16] {'tp'}, dimensions={1} | all-to-all | bytes 8388608 | tf_op jit(solution)/shard_map/all_to_all | solution.py:25
  323.2 35.5 %all-gather.13.cloned.1.call-done = bf16[1,1024,2048]{2,1,0:T(8,128)(2,1)} async-done(((bf16[1,64,2048]{2,1,0:T(8,128)(2,1)}), bf16[1,1024,2048]{2,1,0:T(8,128)(2,1)}) %all-gather.13.cloned.1.call-update) | async-done | bytes 4194320 | tf_op jit(solution)/shard_map/all_gather | solution.py:19
  358.7 3.7 fusion.178
  370.4 100.0 %all_to_all.41 = bf16[1,16,64,2048]{3,2,0,1:T(8,128)(2,1)S(1)} all-to-all(bf16[1,16,64,2048]{3,2,0,1:T(8,128)(2,1)S(1)} %bitcast.437), channel_id=1, replica_groups=mesh['dp'=4,'tp'=16] {'tp'}, dimensions={1} | all-to-all | bytes 8388608 | tf_op jit(solution)/shard_map/all_to_all | solution.py:25
  473.8 34.9 %all-gather.15.cloned.1.call-done = bf16[1,1024,2048]{2,1,0:T(8,128)(2,1)} async-done(((bf16[1,64,2048]{2,1,0:T(8,128)(2,1)}), bf16[1,1024,2048]{2,1,0:T(8,128)(2,1)}) %all-gather.15.cloned.1.call-update) | async-done | bytes 4194320 | tf_op jit(solution)/shard_map/all_gather | solution.py:19
  508.7 6.5 fusion.24
  515.2 31.9 %all-gather.17.cloned.1.call-done = bf16[1,1024,2048]{2,1,0:T(8,128)(2,1)} async-done(((bf16[1,64,2048]{2,1,0:T(8,128)(2,1)}), bf16[1,1024,2048]{2,1,0:T(8,128)(2,1)}) %all-gather.17.cloned.1.call-update) | async-done | bytes 4194320 | tf_op jit(solution)/shard_map/all_gather | solution.py:19
  547.0 7.2 fusion.254
  554.3 4.4 convolution_convert_fusion.1
  558.6 4.7 all-to-all-start.4
  563.3 6.8 convolution_convert_fusion.2
  570.1 86.3 %all-to-all-done.4 = bf16[1,16,64,2048]{3,2,0,1:T(8,128)(2,1)} async-done(((bf16[1,16,64,2048]{3,2,0,1:T(8,128)(2,1)}), bf16[1,16,64,2048]{3,2,0,1:T(8,128)(2,1)}, u32[]{:S(2)}, u32[]{:S(2)}) %all-to-all-start.4) | async-done | bytes 4194336 | tf_op jit(solution)/shard_map/all_to_all | solution.py:25
  656.5 7.6 all-to-all-start.3
  664.4 3.9 convert_reduce_fusion.6
  669.1 87.8 %all-to-all-done.3 = bf16[1,16,64,2048]{3,2,0,1:T(8,128)(2,1)} async-done(((bf16[1,16,64,2048]{3,2,0,1:T(8,128)(2,1)}), bf16[1,16,64,2048]{3,2,0,1:T(8,128)(2,1)}, u32[]{:S(2)}, u32[]{:S(2)}) %all-to-all-start.3) | async-done | bytes 4194336 | tf_op jit(solution)/shard_map/all_to_all | solution.py:25
  756.9 3.1 convert_reduce_fusion.8
  762.8 41.6 %all-gather.19.cloned.1.call-done = bf16[1,1024,2048]{2,1,0:T(8,128)(2,1)} async-done(((bf16[1,64,2048]{2,1,0:T(8,128)(2,1)}), bf16[1,1024,2048]{2,1,0:T(8,128)(2,1)}) %all-gather.19.cloned.1.call-update) | async-done | bytes 4194320 | tf_op jit(solution)/shard_map/all_gather | solution.py:19
  804.4 3.7 fusion.184
  814.2 1.3 fusion.227
  815.5 2.3 add_convert_fusion.1
  817.8 100.2 %all_to_all.42 = bf16[1,16,64,2048]{3,2,0,1:T(8,128)(2,1)S(1)} all-to-all(bf16[1,16,64,2048]{3,2,0,1:T(8,128)(2,1)S(1)} %bitcast.439), channel_id=1, replica_groups=mesh['dp'=4,'tp'=16] {'tp'}, dimensions={1} | all-to-all | bytes 8388608 | tf_op jit(solution)/shard_map/all_to_all | solution.py:25
  918.1 1.6 convert_reduce_fusion.4
  921.4 35.5 %all-gather.21.cloned.1.call-done = bf16[1,1024,2048]{2,1,0:T(8,128)(2,1)} async-done(((bf16[1,64,2048]{2,1,0:T(8,128)(2,1)}), bf16[1,1024,2048]{2,1,0:T(8,128)(2,1)}) %all-gather.21.cloned.1.call-update) | async-done | bytes 4194320 | tf_op jit(solution)/shard_map/all_gather | solution.py:19
  956.8 7.2 fusion.255
  964.1 2.4 convolution_convert_fusion
  966.5 100.0 %all_to_all.43 = bf16[1,16,64,2048]{3,2,0,1:T(8,128)(2,1)S(1)} all-to-all(bf16[1,16,64,2048]{3,2,0,1:T(8,128)(2,1)S(1)} %bitcast.443), channel_id=1, replica_groups=mesh['dp'=4,'tp'=16] {'tp'}, dimensions={1} | all-to-all | bytes 8388608 | tf_op jit(solution)/shard_map/all_to_all | solution.py:25
  1066.5 1.6 convert_reduce_fusion.2
  1069.7 35.5 %all-gather.23.cloned.1.call-done = bf16[1,1024,2048]{2,1,0:T(8,128)(2,1)} async-done(((bf16[1,64,2048]{2,1,0:T(8,128)(2,1)}), bf16[1,1024,2048]{2,1,0:T(8,128)(2,1)}) %all-gather.23.cloned.1.call-update) | async-done | bytes 4194320 | tf_op jit(solution)/shard_map/all_gather | solution.py:19
  1105.2 3.5 fusion.187
  1113.5 1.3 fusion.226
  1114.8 1.3 fusion.225
  1116.1 3.2 add_convert_fusion
  1119.4 4.8 all-to-all-start.7
  1124.5 4.7 fusion.74
  1129.2 2.7 fusion.71
  1132.0 1.3 fusion.112
  1133.3 1.3 fusion.118
  1134.7 1.3 fusion.115
  1136.9 1.5 fusion.109
  1139.0 2.5 fusion.77
  1141.5 2.5 pad_maximum_fusion
  1145.8 2.9 fusion.68
  1148.8 2.4 pad_maximum_fusion.1
  1151.2 104.9 %psum.15 = f32[2,2,2048]{2,1,0:T(2,128)} all-reduce(f32[2,2,2048]{2,1,0:T(2,128)S(1)} %pad_maximum_fusion.4), channel_id=1, replica_groups=mesh['dp'=4,'tp'=16] {'tp'}, use_global_device_ids=true, to_apply=%region_43.44 | all-reduce | flops 8192 | bytes 65536 | tf_op jit(solution)/shard_map/psum | solution.py:113
  1256.2 3.1 fusion.106
  1260.3 1.3 fusion.121
  1261.7 1.3 fusion.127
  1263.0 1.3 fusion.124
  1264.5 1.9 maximum_bitcast_fusion
  1266.5 3.9 convert_reduce_fusion
  1272.7 104.1 %all-reduce.2.cloned.1.call-done = f32[2,4,2048]{2,1,0:T(4,128)} async-done(((f32[2,4,2048]{2,1,0:T(4,128)}), f32[2,4,2048]{2,1,0:T(4,128)}) %all-reduce.2.cloned.1.call-update) | async-done | bytes 65552 | tf_op jit(solution)/shard_map/psum | solution.py:113
  1376.8 1.5 copy.29
  (244 shorter events, 48.6 us)
Async XLA Ops:
  7.2 49.7 %all-gather.9.cloned.1.call-start = ((), (), s32[]{:S(2)}) async-start(), calls=%async_computation.8 | async-start | bytes 4456448 | tf_op jit(solution)/shard_map/all_gather | solution.py:19
  8.4 52.1 %copy-start.54 = (f32[64]{0:T(128)}, f32[64]{0:T(128)S(1)}, u32[]{:S(2)}) copy-start(f32[64]{0:T(128)S(1)} %broadcast_multiply_fusion.3) | copy-start | bytes 772
  10.1 50.4 %copy-start.56 = (f32[64]{0:T(128)}, f32[64]{0:T(128)S(1)}, u32[]{:S(2)}) copy-start(f32[64]{0:T(128)S(1)} %fusion.233) | copy-start | bytes 772
  16.2 45.5 %copy-start.15 = (bf16[2048,3,1,128]{3,0,1,2:T(8,128)(2,1)}, bf16[2048,3,1,128]{3,0,1,2:T(8,128)(2,1)S(1)}, u32[]{:S(2)}) copy-start(bf16[2048,3,1,128]{3,0,1,2:T(8,128)(2,1)S(1)} %get-tuple-element.62) | copy-start | bytes 4718596
  56.9 3.6 copy-start
  64.4 2.9 copy-start.37
  66.8 3.8 copy-start.39
  67.3 3.3 copy-start.24
  70.6 4.9 copy-start.53
  70.6 97.9 %all-to-all-start = ((bf16[1,16,64,2048]{3,2,0,1:T(8,128)(2,1)}), bf16[1,16,64,2048]{3,2,0,1:T(8,128)(2,1)}, u32[]{:S(2)}, u32[]{:S(2)}) async-start(bf16[1,16,64,2048]{3,2,0,1:T(8,128)(2,1)} %bitcast.436), calls=%async_computation | async-start | bytes 8388608 | tf_op jit(solution)/shard_map/all_to_all | solution.py:25
  75.4 96.2 %copy-start.13 = (bf16[1,64,2048]{2,1,0:T(8,128)(2,1)S(1)}, bf16[1,64,2048]{2,1,0:T(8,128)(2,1)}, u32[]{:S(2)}) copy-start(bf16[1,64,2048]{2,1,0:T(8,128)(2,1)} %param.9) | copy-start | bytes 786436
  75.4 98.0 %copy-start.58 = (f32[2,512]{1,0:T(2,128)S(1)}, f32[2,512]{1,0:T(2,128)}, u32[]{:S(2)}) copy-start(f32[2,512]{1,0:T(2,128)} %param.16) | copy-start | bytes 12292
  75.4 137.7 %all-gather.11.cloned.1.call-start = ((), (), s32[]{:S(2)}) async-start(), calls=%async_computation.9 | async-start | bytes 4456448 | tf_op jit(solution)/shard_map/all_gather | solution.py:19
  172.9 185.8 %all-gather.13.cloned.1.call-start = ((), (), s32[]{:S(2)}) async-start(), calls=%async_computation.10 | async-start | bytes 4456448 | tf_op jit(solution)/shard_map/all_gather | solution.py:19
  213.2 5.3 copy-start.61
  218.5 2.6 copy-start.67
  323.1 185.6 %all-gather.15.cloned.1.call-start = ((), (), s32[]{:S(2)}) async-start(), calls=%async_computation.11 | async-start | bytes 4456448 | tf_op jit(solution)/shard_map/all_gather | solution.py:19
  358.7 3.7 copy-start.2
  358.7 4.1 copy-start.17
  366.7 2.4 copy-start.8
  366.7 2.4 copy-start.38
  473.1 73.9 %all-gather.17.cloned.1.call-start = ((), (), s32[]{:S(2)}) async-start(), calls=%async_computation.12 | async-start | bytes 4456448 | tf_op jit(solution)/shard_map/all_gather | solution.py:19
  547.0 7.2 copy-start.62
  554.2 4.4 copy-start.70
  558.6 97.8 %all-to-all-start.4 = ((bf16[1,16,64,2048]{3,2,0,1:T(8,128)(2,1)}), bf16[1,16,64,2048]{3,2,0,1:T(8,128)(2,1)}, u32[]{:S(2)}, u32[]{:S(2)}) async-start(bf16[1,16,64,2048]{3,2,0,1:T(8,128)(2,1)} %bitcast.441), calls=%async_computation.4 | async-start | bytes 8388608 | tf_op jit(solution)/shard_map/all_to_all | solution.py:25
  656.5 100.4 %all-to-all-start.3 = ((bf16[1,16,64,2048]{3,2,0,1:T(8,128)(2,1)}), bf16[1,16,64,2048]{3,2,0,1:T(8,128)(2,1)}, u32[]{:S(2)}, u32[]{:S(2)}) async-start(bf16[1,16,64,2048]{3,2,0,1:T(8,128)(2,1)} %bitcast.440), calls=%async_computation.3 | async-start | bytes 8388608 | tf_op jit(solution)/shard_map/all_to_all | solution.py:25
  664.1 140.3 %all-gather.19.cloned.1.call-start = ((), (), s32[]{:S(2)}) async-start(), calls=%async_computation.13 | async-start | bytes 4456448 | tf_op jit(solution)/shard_map/all_gather | solution.py:19
  664.4 3.9 copy-start.11
  756.9 3.1 copy-start.12
  756.9 3.1 copy-start.20
  756.9 4.9 copy-start.34
  762.7 194.1 %all-gather.21.cloned.1.call-start = ((), (), s32[]{:S(2)}) async-start(), calls=%async_computation.14 | async-start | bytes 4456448 | tf_op jit(solution)/shard_map/all_gather | solution.py:19
  804.4 3.7 copy-start.9
  804.4 4.6 copy-start.42
  808.1 2.3 copy-start.7
  809.0 6.5 copy-start.30
  918.1 2.2 copy-start.35
  921.3 183.9 %all-gather.23.cloned.1.call-start = ((), (), s32[]{:S(2)}) async-start(), calls=%async_computation.15 | async-start | bytes 4456448 | tf_op jit(solution)/shard_map/all_gather | solution.py:19
  956.8 7.2 copy-start.63
  964.0 2.4 copy-start.72
  1069.6 40.0 %copy-start.40 = (bf16[1024,128]{1,0:T(8,128)(2,1)S(1)}, bf16[1024,128]{1,0:T(8,128)(2,1)}, u32[]{:S(2)}) copy-start(bf16[1024,128]{1,0:T(8,128)(2,1)} %copy-done.39) | copy-start | bytes 786436
  1108.8 2.3 copy-start.5
  1109.6 6.5 copy-start.32
  1119.3 5.1 copy-start.71
  1119.4 147.1 %all-to-all-start.7 = ((bf16[1,16,64,2048]{3,2,0,1:T(8,128)(2,1)}), bf16[1,16,64,2048]{3,2,0,1:T(8,128)(2,1)}, u32[]{:S(2)}, u32[]{:S(2)}) async-start(bf16[1,16,64,2048]{3,2,0,1:T(8,128)(2,1)} %bitcast.438), calls=%async_computation.7 | async-start | bytes 8388608 | tf_op jit(solution)/shard_map/all_to_all | solution.py:25
  1124.2 252.7 %all-reduce.2.cloned.1.call-start = ((), (), s32[]{:S(2)}) async-start(), calls=%async_computation.16 | async-start | bytes 131072 | tf_op jit(solution)/shard_map/psum | solution.py:113
  1124.5 4.7 copy-start.65
  1124.5 4.7 copy-start.69
  1129.2 2.7 copy-start.3
  1129.2 2.7 copy-start.31
  1132.0 2.7 copy-start.27
  1136.0 3.0 copy-start.64
  1136.0 3.0 copy-start.73
  1141.5 3.7 copy-start.66
  1141.5 4.4 copy-start.68
  1148.8 107.4 %copy-start.25 = (bf16[1024,128]{0,1:T(8,128)(2,1)S(1)}, bf16[1024,128]{0,1:T(8,128)(2,1)}, u32[]{:S(2)}) copy-start(bf16[1024,128]{0,1:T(8,128)(2,1)} %copy-done.24) | copy-start | bytes 786436
  1151.2 109.1 %copy-start.33 = (bf16[1024,128]{0,1:T(8,128)(2,1)S(1)}, bf16[1024,128]{0,1:T(8,128)(2,1)}, u32[]{:S(2)}) copy-start(bf16[1024,128]{0,1:T(8,128)(2,1)} %copy-done.32) | copy-start | bytes 786436
  1256.2 3.1 copy-start.36
  1256.2 4.1 copy-start.1
  1264.5 5.9 copy-start.14
  1264.5 5.8 copy-start.52
  1264.5 5.8 copy-start.55
  1266.5 4.1 copy-start.60
  1266.5 4.2 copy-start.57
  (23 other events, 32.6 us)
Sparse Core Ops, SparseCore 0:
  13.1 43.6 all-gather.8
  173.0 40.0 all-gather.10
  323.2 35.3 all-gather.12
  473.2 35.3 all-gather.14
  510.2 36.8 all-gather.16
  762.8 41.4 all-gather.18
  921.4 35.3 all-gather.20
  1069.8 35.3 all-gather.22
  1271.9 104.8 all-reduce.1
where the time goes:
time: 1390 us
  waiting for transfers between devices  667 us (48%)
  blocking collectives  505 us (36%)
  matrix products  112 us (8%)
  other arithmetic  47.2 us (3%)
  starting transfers between devices  23.3 us (2%)
  between operations  15.5 us (1%)
  local copies, waits for them, and re-layouts  15 us (1%)
    all_to_all x4, blocking collectives, scatter_rows(): received = lax.all_to_all(sent, 'tp', 1, 1, tiled=True)  400 us
    all_gather x8, waiting for transfers between devices, gather_rows(): return lax.all_gather(local_vals, 'tp', axis=1, tiled=True)  295 us
    all_to_all x4, waiting for transfers between devices, scatter_rows(): received = lax.all_to_all(sent, 'tp', 1, 1, tiled=True)  267 us
    psum x1, blocking collectives, device_step(): lax.psum((jnp.stack([grad_set[0] for grad_set in layer_grads]), jnp.stack...  105 us
    psum x1, waiting for transfers between devices, device_step(): lax.psum((jnp.stack([grad_set[0] for grad_set in layer_grads]), jnp.stack...  104 us
  transfers between devices with their start and end apart: 13, of which 12 were waited for; matrix products, arithmetic and copies ran while one was open for 4% of the time, Pallas kernels for 0%

commit v1 on v0

v1 whole, which is shorter than its diff:
```python
import functools

import jax
import jax.numpy as jnp
from jax import lax
from jax.experimental import pallas as pl
from jax.experimental.pallas import tpu as pltpu
from jax.sharding import PartitionSpec as P

F32 = jnp.float32
BF16 = jnp.bfloat16
MESH = pl.DeviceIdType.MESH


class Ring:
    def __init__(self, n):
        self.n = n
        self.nz = n // 2
        self.me = lax.axis_index('tp')
        self.z = self.me // 2
        self.c = lax.rem(self.me, 2)
        self.sib = self.me + 1 - 2 * self.c
        self.next = {1: lax.rem(self.me + 2, n), -1: lax.rem(self.me + n - 2, n)}

    def chip(self, off):
        return lax.rem(self.z + (off + self.nz), self.nz)

    def enter(self):
        bar = pltpu.get_barrier_semaphore()
        for dev in (self.next[1], self.next[-1], self.sib):
            pl.semaphore_signal(bar, inc=1, device_id={'tp': dev}, device_id_type=MESH)
        pl.semaphore_wait(bar, 3)


def remote(src, dst, send_sem, recv_sem, dev):
    return pltpu.make_async_remote_copy(src_ref=src, dst_ref=dst, send_sem=send_sem, recv_sem=recv_sem,
                                        device_id={'tp': dev}, device_id_type=MESH)


def gather_pieces(ring):
    far = ring.nz // 2
    out = []
    for k in range(far):
        for h in range(2):
            for d in (1, -1):
                if k < far - 1 or h == (0 if d == 1 else 1):
                    out.append((d, k, h))
    return out


def ring_gather(ring, own_ref, all_ref, send_sem, recv_sem, psend, precv, on_hop=None):
    rows = own_ref.shape[0]
    half = rows // 2
    far = ring.nz // 2

    def piece(off, core, h):
        return all_ref.at[ring.chip(off), pl.ds(pl.multiple_of(core * rows + h * half, half), half)]

    def forward(d, k, h):
        dst = piece(-d * k, ring.c, h)
        src = own_ref.at[pl.ds(h * half, half)] if k == 0 else dst
        return remote(src, dst, send_sem.at[(1 - d) // 2, k, h], recv_sem.at[(1 - d) // 2, k, h], ring.next[d])

    def arrival(d, k, h):
        ref = piece(-d * (k + 1), ring.c, h)
        return remote(ref, ref, send_sem.at[(1 - d) // 2, k, h], recv_sem.at[(1 - d) // 2, k, h], ring.next[d])

    def pair(d, k, h, core):
        ref = piece(-d * (k + 1), core, h)
        return remote(ref, ref, psend.at[(1 - d) // 2, k, h], precv.at[(1 - d) // 2, k, h], ring.sib)

    def own_pair(core):
        ref = all_ref.at[ring.z, pl.ds(pl.multiple_of(core * rows, rows), rows)]
        return remote(own_ref, ref, psend.at[0, far, 0], precv.at[0, far, 0], ring.sib)

    order = gather_pieces(ring)
    for h in range(2):
        for d in (1, -1):
            forward(d, 0, h).start()
    own_pair(ring.c).start()
    all_ref[ring.z, pl.ds(pl.multiple_of(ring.c * rows, rows), rows)] = own_ref[...]
    own_pair(1 - ring.c).wait_recv()
    if on_hop is not None:
        on_hop((0,))
    for k in range(far):
        mine = [p for p in order if p[1] == k]
        for d, _, h in mine:
            arrival(d, k, h).wait_recv()
            if (d, k + 1, h) in order:
                forward(d, k + 1, h).start()
            pair(d, k, h, ring.c).start()
        for d, _, h in mine:
            pair(d, k, h, 1 - ring.c).wait_recv()
        if on_hop is not None:
            on_hop((k + 1, -(k + 1)) if k < far - 1 else (far,))
    for d, k, h in order:
        forward(d, k, h).wait_send()
        pair(d, k, h, ring.c).wait_send()
    own_pair(ring.c).wait_send()


def scatter_offsets(ring):
    far = ring.nz // 2
    offs = [far]
    for k in range(far - 1, 0, -1):
        offs += [k, -k]
    return offs + [0]


def ring_scatter(ring, own_part, give_ref, pair_ref, send_ref, recv_ref, send_sem, recv_sem, psend, precv, make=None):
    far = ring.nz // 2
    offs = scatter_offsets(ring)
    half = recv_ref.shape[2]
    slots = {}
    for d in (1, -1):
        hd = 0 if d == 1 else 1
        lst = [(far, hd)]
        for k in range(far - 1, 0, -1):
            lst += [(k, 1 - hd), (k, hd)]
        slots[d] = lst

    def pair(j):
        return remote(give_ref(j), pair_ref.at[j], psend.at[j], precv.at[j], ring.sib)

    def hop(d, s):
        i = (1 - d) // 2
        return remote(send_ref.at[i, s], recv_ref.at[i, s], send_sem.at[i, s], recv_sem.at[i, s], ring.next[d])

    made = set()

    def need(j):
        while len(made) <= j:
            i = len(made)
            if make is not None:
                make(i, offs[i])
            pair(i).start()
            made.add(i)

    paired = set()

    def base(j, h):
        need(min(j + 2, len(offs) - 1))
        if j not in paired:
            pair(j).wait_recv()
            paired.add(j)
        return own_part(j, h) + pair_ref[j, pl.ds(h * half, half)].astype(F32)

    need(0)
    for s in range(len(slots[1])):
        for d in (1, -1):
            k, h = slots[d][s]
            val = base(offs.index(d * k if k < far else far), h)
            if s >= 2:
                hop(d, s - 2).wait_recv()
                val = val + recv_ref[(1 - d) // 2, s - 2].astype(F32)
            send_ref[(1 - d) // 2, s] = val.astype(BF16)
            hop(d, s).start()
    last = len(slots[1])
    got = set()

    def total(h):
        val = base(len(offs) - 1, h)
        for d in (1, -1):
            s = last - 1 if slots[d][last - 1][1] == h else last - 2
            if (d, s) not in got:
                hop(d, s).wait_recv()
                got.add((d, s))
            val = val + recv_ref[(1 - d) // 2, s].astype(F32)
        return val

    def finish():
        for d in (1, -1):
            for s in range(last):
                hop(d, s).wait_send()
        for j in range(len(offs)):
            pair(j).wait_send()

    return total, finish


def gather_sems(n):
    far = n // 4
    return [pltpu.SemaphoreType.DMA((2, far + 1, 2)) for _ in range(4)]


def scatter_sems(n):
    steps = n // 2 - 1
    return [pltpu.SemaphoreType.DMA((2, steps)), pltpu.SemaphoreType.DMA((2, steps)),
            pltpu.SemaphoreType.DMA((n // 2,)), pltpu.SemaphoreType.DMA((n // 2,))]


VM = pl.BlockSpec(memory_space=pltpu.VMEM)


def comm_params(cid):
    return pltpu.CompilerParams(collective_id=cid, has_side_effects=True, vmem_limit_bytes=60 * 1024 * 1024)


def gather_rows(local, n):
    rows, width = local.shape

    def body(own_ref, all_ref, *sems):
        ring = Ring(n)
        ring.enter()
        ring_gather(ring, own_ref, all_ref, *sems)

    out = pl.pallas_call(
        body, out_shape=jax.ShapeDtypeStruct((n // 2, 2 * rows, width), BF16), in_specs=[VM], out_specs=VM,
        scratch_shapes=gather_sems(n), compiler_params=comm_params(1), name='ring_gather')(local)
    return out.reshape(n * rows, width)


def scatter_rows(partial, n):
    total_rows, width = partial.shape
    rows = total_rows // n
    half = rows // 2
    parts = partial.astype(BF16).reshape(n // 2, 2 * rows, width)

    def body(part_ref, out_ref, pair_ref, send_ref, recv_ref, *sems):
        ring = Ring(n)
        offs = scatter_offsets(ring)
        ring.enter()

        def own_part(j, h):
            at = pl.multiple_of(ring.c * rows + h * half, half)
            return part_ref[ring.chip(offs[j]), pl.ds(at, half)].astype(F32)

        def give(j):
            return part_ref.at[ring.chip(offs[j]), pl.ds(pl.multiple_of((1 - ring.c) * rows, rows), rows)]

        total, finish = ring_scatter(ring, own_part, give, pair_ref, send_ref, recv_ref, *sems)
        for h in range(2):
            out_ref[pl.ds(h * half, half)] = total(h)
        finish()

    steps = n // 2 - 1
    return pl.pallas_call(
        body, out_shape=jax.ShapeDtypeStruct((rows, width), F32), in_specs=[VM], out_specs=VM,
        scratch_shapes=[pltpu.VMEM((n // 2, rows, width), BF16), pltpu.VMEM((2, steps, half, width), BF16),
                        pltpu.VMEM((2, steps, half, width), BF16)] + scatter_sems(n),
        compiler_params=comm_params(2), name='ring_scatter')(parts)


def sum_small(vals, n):
    r, width = vals.shape
    cols = width // n
    pad = -r % 8
    blocks = jnp.pad(vals, ((0, pad), (0, 0))).reshape(r + pad, n, cols).transpose(1, 0, 2)

    def body(in_ref, out_ref, got_ref, s1, r1, s2, r2):
        me = lax.axis_index('tp')
        bar = pltpu.get_barrier_semaphore()
        peers = [lax.rem(me + j, n) for j in range(n)]
        for j in range(1, n):
            pl.semaphore_signal(bar, inc=1, device_id={'tp': peers[j]}, device_id_type=MESH)
        pl.semaphore_wait(bar, n - 1)
        first = [None] + [remote(in_ref.at[peers[j]], got_ref.at[j], s1.at[j], r1.at[j], peers[j]) for j in range(1, n)]
        for j in range(1, n):
            first[j].start()
        acc = in_ref[me]
        for j in range(1, n):
            first[j].wait_recv()
            acc = acc + got_ref[j]
        got_ref[0] = acc
        out_ref[me] = acc
        second = [None] + [remote(got_ref.at[0], out_ref.at[me], s2.at[j], r2.at[j], peers[j]) for j in range(1, n)]
        for j in range(1, n):
            second[j].start()
        for j in range(1, n):
            src = lax.rem(me + n - j, n)
            remote(got_ref.at[0], out_ref.at[src], s2.at[j], r2.at[j], peers[j]).wait_recv()
        for j in range(1, n):
            first[j].wait_send()
            second[j].wait_send()

    out = pl.pallas_call(
        body, out_shape=jax.ShapeDtypeStruct(blocks.shape, F32), in_specs=[VM], out_specs=VM,
        scratch_shapes=[pltpu.VMEM(blocks.shape, F32)] + [pltpu.SemaphoreType.DMA((n,))] * 4,
        compiler_params=comm_params(3), name='sum_small')(blocks)
    return out.transpose(1, 0, 2).reshape(r + pad, width)[:r]


def layer_norm(row_vals, ln_gain, ln_shift):
    mean_val = jnp.mean(row_vals, axis=-1, keepdims=True)
    centered = row_vals - mean_val
    var_val = jnp.mean(centered * centered, axis=-1, keepdims=True)
    return centered * lax.rsqrt(var_val + 1e-5) * ln_gain + ln_shift


def gelu_tanh(pre_act):
    return jax.nn.gelu(pre_act, approximate=True)


def mm(spec, a, b):
    return jnp.einsum(spec, a, b, preferred_element_type=F32)


def attention(q, k, v):
    seq_len = q.shape[0]
    scores = mm('qe,ke->qk', q, k) * q.shape[-1] ** -0.5
    positions = jnp.arange(seq_len)
    scores = jnp.where(positions[:, None] >= positions[None, :], scores, -1e30)
    prob = jax.nn.softmax(scores, axis=-1).astype(BF16)
    return mm('qk,ke->qe', prob, v).astype(BF16), prob


def attention_backward(d_attn, q, k, v, prob):
    d_prob = mm('qe,ke->qk', d_attn, v)
    d_v = mm('qk,qe->ke', prob, d_attn)
    row_dot = jnp.sum(d_prob * prob, axis=-1, keepdims=True)
    d_score = (prob * (d_prob - row_dot) * q.shape[-1] ** -0.5).astype(BF16)
    return mm('qk,ke->qe', d_score, k), mm('qk,qe->ke', d_score, q), d_v


def solution(mesh):
    n = mesh.shape['tp']

    def device_step(x_loc, dy_loc, ln_par, bias_d, w_qkv, w_out, w_up, b_up, w_down):
        n_layers = ln_par.shape[0]
        residual = x_loc[0].astype(F32)
        wq = jnp.transpose(w_qkv[:, :, :, 0], (0, 2, 1, 3))
        saved = []
        for l in range(n_layers):
            ln, bias = ln_par[l], bias_d[l]
            res_one = residual
            h_all = gather_rows(layer_norm(res_one, ln[0], ln[1]).astype(BF16), n)
            q, k, v = [mm('sd,de->se', h_all, wq[l, i]).astype(BF16) for i in range(3)]
            attn, prob = attention(q, k, v)
            res_two = res_one + scatter_rows(mm('se,ed->sd', attn, w_out[l, 0]), n) + bias[0]
            h2_all = gather_rows(layer_norm(res_two, ln[2], ln[3]).astype(BF16), n)
            pre_act = mm('sd,df->sf', h2_all, w_up[l]) + b_up[l]
            act_f, gelu_pull = jax.vjp(gelu_tanh, pre_act)
            act = act_f.astype(BF16)
            residual = res_two + scatter_rows(mm('sf,fd->sd', act, w_down[l]), n) + bias[1]
            saved.append((res_one, h_all, q, k, v, prob, attn, res_two, h2_all, gelu_pull, act))
        y_loc = residual.astype(BF16)

        d_res = dy_loc[0].astype(F32)
        grads = [None] * n_layers
        for l in reversed(range(n_layers)):
            res_one, h_all, q, k, v, prob, attn, res_two, h2_all, gelu_pull, act = saved[l]
            ln = ln_par[l]
            d_bias_two = jnp.sum(d_res, axis=0)
            d_all = gather_rows(d_res.astype(BF16), n)
            d_wdown = mm('sf,sd->fd', act, d_all)
            d_pre = gelu_pull(mm('sd,fd->sf', d_all, w_down[l]))[0]
            d_bup = jnp.sum(d_pre, axis=0)
            d_pre_bf = d_pre.astype(BF16)
            d_wup = mm('sd,sf->df', h2_all, d_pre_bf)
            d_h2 = scatter_rows(mm('sf,df->sd', d_pre_bf, w_up[l]), n)
            d_mid, d_g2, d_s2 = jax.vjp(layer_norm, res_two, ln[2], ln[3])[1](d_h2)
            d_res = d_res + d_mid
            d_bias_one = jnp.sum(d_res, axis=0)
            d_all = gather_rows(d_res.astype(BF16), n)
            d_wout = mm('se,sd->ed', attn, d_all)
            d_attn = mm('sd,ed->se', d_all, w_out[l, 0]).astype(BF16)
            d_proj = [g.astype(BF16) for g in attention_backward(d_attn, q, k, v, prob)]
            d_wqkv = jnp.stack([mm('sd,se->de', h_all, g) for g in d_proj], axis=0)
            d_h = scatter_rows(sum(mm('se,de->sd', d_proj[i], wq[l, i]) for i in range(3)), n)
            d_in, d_g1, d_s1 = jax.vjp(layer_norm, res_one, ln[0], ln[1])[1](d_h)
            d_res = d_res + d_in
            grads[l] = (jnp.stack([d_g1, d_s1, d_g2, d_s2, d_bias_one, d_bias_two]), d_wqkv, d_wout, d_wup, d_bup, d_wdown)
        small = sum_small(jnp.concatenate([g[0] for g in grads], axis=0), n)
        small = small.reshape(n_layers, 6, small.shape[-1])
        stacked = [jnp.stack([g[i] for g in grads]) for i in range(1, 6)]
        return (y_loc[None], d_res.astype(BF16)[None], small[:, :4], small[:, 4:],
                jnp.transpose(stacked[0].astype(BF16), (0, 2, 1, 3))[:, :, :, None], stacked[1].astype(BF16)[:, None],
                stacked[2].astype(BF16), stacked[3], stacked[4].astype(BF16))

    in_specs = (P('dp', 'tp', None), P('dp', 'tp', None), P(None, None, None), P(None, None, None),
                P(None, None, None, 'tp', None), P(None, 'tp', None, None), P(None, None, 'tp'), P(None, 'tp'), P(None, 'tp', None))
    out_specs = (P('dp', 'tp', None), P('dp', 'tp', None), P('dp', None, None), P('dp', None, None),
                 P('dp', None, None, 'tp', None), P('dp', 'tp', None, None), P('dp', None, 'tp'), P('dp', 'tp'), P('dp', 'tp', None))
    return jax.shard_map(device_step, mesh=mesh, in_specs=in_specs, out_specs=out_specs, check_vma=False)
```

time: 1390 us -> 692 us (0.50)
  waiting for transfers between devices: 667 us -> 0 us
  Pallas kernels: 0 us -> 506 us
  blocking collectives: 505 us -> 0 us
  starting transfers between devices: 23.3 us -> 0 us
    pallas_call x0 -> x17, Pallas kernels: none -> 497 us  [the longest x8 249 us: gather_rows(): pl.pallas_call(body, out_shape=jax.ShapeDtypeStruct((n // 2, 2 * rows, wi...]
    all_to_all x4 -> x0, blocking collectives: 400 us -> none  [scatter_rows(): received = lax.all_to_all(sent, 'tp', 1, 1, tiled=True)]
    all_gather x8 -> x0, waiting for transfers between devices: 295 us -> none  [gather_rows(): return lax.all_gather(local_vals, 'tp', axis=1, tiled=True)]
    all_to_all x4 -> x0, waiting for transfers between devices: 267 us -> none  [scatter_rows(): received = lax.all_to_all(sent, 'tp', 1, 1, tiled=True)]
    psum x1 -> x0, blocking collectives: 105 us -> none  [device_step(): lax.psum((jnp.stack([grad_set[0] for grad_set in layer_grads]), jnp.stack...]
    psum x1 -> x0, waiting for transfers between devices: 104 us -> none  [device_step(): lax.psum((jnp.stack([grad_set[0] for grad_set in layer_grads]), jnp.stack...]
    all_to_all x4 -> x0, starting transfers between devices: 21.9 us -> none  [scatter_rows(): received = lax.all_to_all(sent, 'tp', 1, 1, tiled=True)]
    dot_general x48 -> x46, matrix products: 112 us -> 117 us  [mm(): return jnp.einsum(spec, a, b, preferred_element_type=F32)]
  transfers between devices with their start and end apart: 13 -> 0, of which waited for: 12 -> 0; matrix products, arithmetic and copies ran while one was open for 4% -> 0% of each run, Pallas kernels for 0% -> 0%
where the time goes in v1:
time: 692 us; the launch traced here: 682 us
  Pallas kernels  506 us (73%)
  matrix products  117 us (17%)
  other arithmetic  40 us (6%)
  local copies, waits for them, and re-layouts  16.1 us (2%)
    pallas_call x8, Pallas kernels, gather_rows(): pl.pallas_call(body, out_shape=jax.ShapeDtypeStruct((n // 2, 2 * rows, wi...  249 us
    pallas_call x8, Pallas kernels, scatter_rows(): pl.pallas_call(body, out_shape=jax.ShapeDtypeStruct((rows, width), F32),...  227 us
    dot_general x46, matrix products, mm(): return jnp.einsum(spec, a, b, preferred_element_type=F32)  117 us
    pallas_call x1, Pallas kernels, sum_small(): pl.pallas_call(body, out_shape=jax.ShapeDtypeStruct(blocks.shape, F32), i...  20.7 us

profile of v1, /device:TPU:21, one launch (start us, length us, event | category | flops | bytes accessed | tf_op | source)
XLA Modules:
  0.0 681.9 jit_solution(4473547225694233037)
XLA Ops:
  5.8 1.8 fusion.65.own_ref
  7.6 36.5 %ring_gather.8 = bf16[8,128,2048]{2,1,0:T(8,128)(2,1)} custom-call(bf16[64,2048]{1,0:T(8,128)(2,1)} %fusion.65.own_ref), custom_call_target="tpu_custom_call" | custom-call | tf_op jit(solution)/shard_map/ring_gather/pallas_call | solution.py:207
  44.2 3.6 convolution_convert_fusion.28
  49.1 2.1 fusion.80
  51.2 29.2 %ring_gather.12 = bf16[8,128,2048]{2,1,0:T(8,128)(2,1)} custom-call(bf16[64,2048]{1,0:T(8,128)(2,1)} %bitcast.305), custom_call_target="tpu_custom_call" | custom-call | tf_op jit(solution)/shard_map/ring_gather/pallas_call | solution.py:207
  81.3 2.0 copy-done.4
  84.3 4.6 online-softmax
  88.8 4.3 convolution_convert_fusion.5
  93.1 28.2 %ring_scatter.8 = f32[64,2048]{1,0:T(8,128)} custom-call(bf16[8,128,2048]{2,1,0:T(8,128)(2,1)} %bitcast.273), custom_call_target="tpu_custom_call" | custom-call | tf_op jit(solution)/shard_map/ring_scatter/pallas_call | solution.py:237
  123.7 31.7 %ring_gather.9 = bf16[8,128,2048]{2,1,0:T(8,128)(2,1)} custom-call(bf16[64,2048]{1,0:T(8,128)(2,1)} %add_convert_fusion.6.own_ref), custom_call_target="tpu_custom_call" | custom-call | tf_op jit(solution)/shard_map/ring_gather/pallas_call | solution.py:207
  155.5 5.3 fusion.42
  160.8 4.6 convolution_convert_fusion.3
  165.5 28.3 %ring_scatter.9 = f32[64,2048]{1,0:T(8,128)} custom-call(bf16[8,128,2048]{2,1,0:T(8,128)(2,1)} %bitcast.284), custom_call_target="tpu_custom_call" | custom-call | tf_op jit(solution)/shard_map/ring_scatter/pallas_call | solution.py:237
  196.1 29.7 %ring_gather.10 = bf16[8,128,2048]{2,1,0:T(8,128)(2,1)} custom-call(bf16[64,2048]{1,0:T(8,128)(2,1)} %add_convert_fusion.5.own_ref), custom_call_target="tpu_custom_call" | custom-call | tf_op jit(solution)/shard_map/ring_gather/pallas_call | solution.py:207
  225.8 3.7 convolution_convert_fusion.26
  229.5 2.4 convolution_convert_fusion.27
  231.9 3.2 fusion.83
  235.9 2.0 copy-done.6
  239.0 4.7 online-softmax.1
  243.7 4.3 convolution_convert_fusion.4
  248.0 28.4 %ring_scatter.10 = f32[64,2048]{1,0:T(8,128)} custom-call(bf16[8,128,2048]{2,1,0:T(8,128)(2,1)} %bitcast.274), custom_call_target="tpu_custom_call" | custom-call | tf_op jit(solution)/shard_map/ring_scatter/pallas_call | solution.py:237
  278.7 31.7 %ring_gather.11 = bf16[8,128,2048]{2,1,0:T(8,128)(2,1)} custom-call(bf16[64,2048]{1,0:T(8,128)(2,1)} %add_convert_fusion.4.own_ref), custom_call_target="tpu_custom_call" | custom-call | tf_op jit(solution)/shard_map/ring_gather/pallas_call | solution.py:207
  310.4 5.3 fusion.36
  315.7 3.6 fusion.120
  319.4 4.0 fusion.11
  323.4 3.9 fusion.9
  327.3 4.6 convolution_convert_fusion.2
  331.9 28.3 %ring_scatter.11 = f32[64,2048]{1,0:T(8,128)} custom-call(bf16[8,128,2048]{2,1,0:T(8,128)(2,1)} %bitcast.281), custom_call_target="tpu_custom_call" | custom-call | tf_op jit(solution)/shard_map/ring_scatter/pallas_call | solution.py:237
  360.2 6.0 convolution_convert_fusion.1
  366.2 28.7 %ring_scatter.12 = f32[64,2048]{1,0:T(8,128)} custom-call(bf16[8,128,2048]{2,1,0:T(8,128)(2,1)} %bitcast.282), custom_call_target="tpu_custom_call" | custom-call | tf_op jit(solution)/shard_map/ring_scatter/pallas_call | solution.py:237
  394.9 1.4 multiply_reduce_fusion
  396.3 2.0 fusion.110
  399.2 30.2 %ring_gather.13 = bf16[8,128,2048]{2,1,0:T(8,128)(2,1)} custom-call(bf16[64,2048]{1,0:T(8,128)(2,1)} %fusion.103.own_ref), custom_call_target="tpu_custom_call" | custom-call | tf_op jit(solution)/shard_map/ring_gather/pallas_call | solution.py:207
  429.4 3.1 fusion.19
  435.1 1.7 fusion
  440.8 1.3 fusion.15
  442.1 1.3 fusion.16
  443.5 2.1 fusion.17
  448.2 3.3 add_convert_fusion.1
  451.4 28.3 %ring_scatter.13 = f32[64,2048]{1,0:T(8,128)} custom-call(bf16[8,128,2048]{2,1,0:T(8,128)(2,1)} %bitcast.279), custom_call_target="tpu_custom_call" | custom-call | tf_op jit(solution)/shard_map/ring_scatter/pallas_call | solution.py:237
  479.7 1.4 multiply_reduce_fusion.1
  481.1 1.3 fusion.109
  483.5 30.6 %ring_gather.14 = bf16[8,128,2048]{2,1,0:T(8,128)(2,1)} custom-call(bf16[64,2048]{1,0:T(8,128)(2,1)} %convert_element_type.188.own_ref), custom_call_target="tpu_custom_call" | custom-call | tf_op jit(solution)/shard_map/ring_gather/pallas_call | solution.py:207
  514.1 7.2 %fusion.121 = (f32[512]{0:T(512)S(1)}, bf16[1024,512]{1,0:T(8,128)(2,1)S(1)}) fusion(f32[1024,512]{1,0:T(8,128)} %copy-done.49, f32[512]{0:T(512)S(1)} %bitcast.341, bf16[1024,2048]{1,0:T(8,128)(2,1)} %bitcast.291, bf16[2,512,2048]{2,1,0:T(8,128)(2,1)} %param.17), kind=kOutput, calls=%fused_computation.222 | convolution fusion | flops 2159017472 | bytes 9441280 | tf_op jit(solution)/shard_map/sd,fd->sf/dot_general | solution.py:295
  521.3 2.7 fusion.10
  524.0 2.5 fusion.8
  527.1 2.4 pad_maximum_fusion
  529.5 2.5 pad_maximum_fusion.1
  533.2 4.6 convolution_convert_fusion
  537.7 28.3 %ring_scatter.14 = f32[64,2048]{1,0:T(8,128)} custom-call(bf16[8,128,2048]{2,1,0:T(8,128)(2,1)} %bitcast.283), custom_call_target="tpu_custom_call" | custom-call | tf_op jit(solution)/shard_map/ring_scatter/pallas_call | solution.py:237
  566.0 1.4 multiply_reduce_fusion.2
  567.4 1.3 fusion.108
  569.7 29.7 %ring_gather.15 = bf16[8,128,2048]{2,1,0:T(8,128)(2,1)} custom-call(bf16[64,2048]{1,0:T(8,128)(2,1)} %convert_element_type.192.own_ref), custom_call_target="tpu_custom_call" | custom-call | tf_op jit(solution)/shard_map/ring_gather/pallas_call | solution.py:207
  599.4 3.1 fusion.18
  605.6 1.3 fusion.3
  610.8 1.3 fusion.12
  612.1 1.6 fusion.13
  613.8 1.3 fusion.14
  615.5 1.9 maximum_bitcast_fusion
  621.0 3.2 add_convert_fusion
  624.2 28.5 %ring_scatter.15 = f32[64,2048]{1,0:T(8,128)} custom-call(bf16[8,128,2048]{2,1,0:T(8,128)(2,1)} %bitcast.280), custom_call_target="tpu_custom_call" | custom-call | tf_op jit(solution)/shard_map/ring_scatter/pallas_call | solution.py:237
  654.0 1.6 fusion.66
  655.6 2.0 fusion.89
  658.4 20.7 %sum_small.1 = f32[16,16,128]{2,1,0:T(8,128)} custom-call(f32[16,16,128]{2,1,0:T(8,128)} %bitcast_bitcast_fusion.in_ref), custom_call_target="tpu_custom_call" | custom-call | tf_op jit(solution)/shard_map/sum_small/pallas_call | solution.py:276
  (164 shorter events, 46.0 us)
Async XLA Ops:
  0.6 43.5 %copy-start.18 = (bf16[2,2048,3,1,128]{4,1,3,2,0:T(8,128)(2,1)S(1)}, bf16[2,2048,3,1,128]{4,1,3,2,0:T(8,128)(2,1)}, u32[]{:S(2)}) copy-start(bf16[2,2048,3,1,128]{4,1,3,2,0:T(8,128)(2,1)} %param.13) | copy-start | bytes 9437188
  1.9 45.9 %copy-start.40 = (f32[64]{0:T(128)}, f32[64]{0:T(128)S(1)}, u32[]{:S(2)}) copy-start(f32[64]{0:T(128)S(1)} %broadcast_multiply_fusion.3) | copy-start | bytes 772
  3.1 1.6 copy-start.44
  3.1 44.7 %copy-start.42 = (f32[64]{0:T(128)}, f32[64]{0:T(128)S(1)}, u32[]{:S(2)}) copy-start(f32[64]{0:T(128)S(1)} %fusion.98) | copy-start | bytes 772
  5.8 38.4 %copy-start.38 = (f32[1,1,2048]{2,1,0:T(1,128)}, f32[1,1,2048]{2,1,0:T(1,128)S(1)}, u32[]{:S(2)}) copy-start(f32[1,1,2048]{2,1,0:T(1,128)S(1)} %get-tuple-element.71) | copy-start | bytes 24580
  44.2 3.6 copy-start
  47.8 32.6 %copy-start.30 = (bf16[1024,128]{1,0:T(8,128)(2,1)}, bf16[1024,128]{1,0:T(8,128)(2,1)S(1)}, u32[]{:S(2)}) copy-start(bf16[1024,128]{1,0:T(8,128)(2,1)S(1)} %convolution_convert_fusion.28) | copy-start | bytes 786436
  49.1 31.4 %copy-start.32 = (bf16[1024,128]{1,0:T(8,128)(2,1)}, bf16[1024,128]{1,0:T(8,128)(2,1)S(1)}, u32[]{:S(2)}) copy-start(bf16[1024,128]{1,0:T(8,128)(2,1)S(1)} %convolution_convert_fusion.29) | copy-start | bytes 786436
  81.2 2.0 copy-start.4
  84.3 4.6 copy-start.26
  93.1 28.3 %copy-start.10 = (bf16[1,64,2048]{2,1,0:T(8,128)(2,1)S(1)}, bf16[1,64,2048]{2,1,0:T(8,128)(2,1)}, u32[]{:S(2)}) copy-start(bf16[1,64,2048]{2,1,0:T(8,128)(2,1)} %param.9) | copy-start | bytes 786436
  155.5 5.4 copy-start.46
  160.8 4.6 copy-start.49
  225.8 3.7 copy-start.2
  229.5 5.6 copy-start.34
  231.9 3.2 copy-start.36
  235.9 2.0 copy-start.6
  310.4 5.4 copy-start.15
  310.4 5.4 copy-start.47
  319.4 4.0 copy-start.16
  366.2 30.1 %copy-start.22 = (f32[64,2048]{1,0:T(8,128)S(1)}, f32[64,2048]{1,0:T(8,128)}, u32[]{:S(2)}) copy-start(f32[64,2048]{1,0:T(8,128)} %ring_scatter.11) | copy-start | bytes 1572868
  366.2 32.2 %copy-start.21 = (bf16[1,64,2048]{2,1,0:T(8,128)(2,1)S(1)}, bf16[1,64,2048]{2,1,0:T(8,128)(2,1)}, u32[]{:S(2)}) copy-start(bf16[1,64,2048]{2,1,0:T(8,128)(2,1)} %param.10) | copy-start | bytes 786436
  398.3 31.1 %copy-start.13 = (f32[1024,128]{1,0:T(8,128)S(1)}, f32[1024,128]{1,0:T(8,128)}, u32[]{:S(2)}) copy-start(f32[1024,128]{1,0:T(8,128)} %online-softmax.1) | copy-start | bytes 1572868
  429.4 3.5 copy-start.8
  432.8 2.2 copy-start.7
  432.8 2.3 copy-start.29
  437.6 1.0 copy-start.37
  437.7 1.7 copy-start.35
  438.6 2.2 copy-start.3
  443.5 2.2 copy-start.19
  514.1 7.2 %copy-start.17 = (bf16[8,128,2048]{2,1,0:T(8,128)(2,1)S(1)}, bf16[8,128,2048]{2,1,0:T(8,128)(2,1)}, u32[]{:S(2)}) copy-start(bf16[8,128,2048]{2,1,0:T(8,128)(2,1)} %ring_gather.14) | copy-start | bytes 12582916
  514.1 7.2 %copy-start.50 = (f32[1024,512]{1,0:T(8,128)S(1)}, f32[1024,512]{1,0:T(8,128)}, u32[]{:S(2)}) copy-start(f32[1024,512]{1,0:T(8,128)} %copy-done.49) | copy-start | bytes 6291460
  521.3 2.7 copy-start.14
  524.0 3.1 copy-start.24
  527.1 2.4 copy-start.23
  529.5 3.7 copy-start.48
  568.8 30.6 %copy-start.12 = (f32[1024,128]{1,0:T(8,128)S(1)}, f32[1024,128]{1,0:T(8,128)}, u32[]{:S(2)}) copy-start(f32[1024,128]{1,0:T(8,128)} %online-softmax) | copy-start | bytes 1572868
  599.4 3.5 copy-start.9
  599.4 3.7 copy-start.27
  603.1 2.3 copy-start.5
  603.2 2.4 copy-start.28
  607.7 1.0 copy-start.33
  607.7 1.7 copy-start.31
  608.6 2.2 copy-start.1
  613.8 1.3 copy-start.25
  615.5 3.0 copy-start.20
  624.2 28.5 %copy-start.11 = (bf16[1,64,2048]{2,1,0:T(8,128)(2,1)S(1)}, bf16[1,64,2048]{2,1,0:T(8,128)(2,1)}, u32[]{:S(2)}) copy-start(bf16[1,64,2048]{2,1,0:T(8,128)(2,1)} %param.9) | copy-start | bytes 786436
  624.2 28.5 %copy-start.39 = (f32[1,1,2048]{2,1,0:T(1,128)S(1)}, f32[1,1,2048]{2,1,0:T(1,128)}, u32[]{:S(2)}) copy-start(f32[1,1,2048]{2,1,0:T(1,128)} %copy-done.38) | copy-start | bytes 24580
  624.2 28.5 %copy-start.41 = (f32[64]{0:T(128)S(1)}, f32[64]{0:T(128)}, u32[]{:S(2)}) copy-start(f32[64]{0:T(128)} %copy-done.40) | copy-start | bytes 772
  624.2 29.8 %copy-start.45 = (f32[64]{0:T(128)S(1)}, f32[64]{0:T(128)}, u32[]{:S(2)}) copy-start(f32[64]{0:T(128)} %copy-done.44) | copy-start | bytes 772
  624.2 29.8 %copy-start.43 = (f32[64]{0:T(128)S(1)}, f32[64]{0:T(128)}, u32[]{:S(2)}) copy-start(f32[64]{0:T(128)} %copy-done.42) | copy-start | bytes 772

commit v2 on v1

v2 whole, which is shorter than its diff:
```python
import math
import types

import jax
import jax.numpy as jnp
from jax import lax
from jax.experimental import pallas as pl
from jax.experimental.pallas import tpu as pltpu
from jax.sharding import PartitionSpec as P

F32 = jnp.float32
BF16 = jnp.bfloat16
MESH = pl.DeviceIdType.MESH


class Ring:
    def __init__(self, n):
        self.n = n
        self.nz = n // 2
        self.me = lax.axis_index('tp')
        self.z = self.me // 2
        self.c = lax.rem(self.me, 2)
        self.sib = self.me + 1 - 2 * self.c
        self.next = {1: lax.rem(self.me + 2, n), -1: lax.rem(self.me + n - 2, n)}

    def chip(self, off):
        return lax.rem(self.z + (off + self.nz), self.nz)

    def enter(self):
        bar = pltpu.get_barrier_semaphore()
        for dev in (self.next[1], self.next[-1], self.sib):
            pl.semaphore_signal(bar, inc=1, device_id={'tp': dev}, device_id_type=MESH)
        pl.semaphore_wait(bar, 3)


def remote(src, dst, send_sem, recv_sem, dev):
    return pltpu.make_async_remote_copy(src_ref=src, dst_ref=dst, send_sem=send_sem, recv_sem=recv_sem,
                                        device_id={'tp': dev}, device_id_type=MESH)


PIECES = 4


def side(d):
    return (1 - d) // 2


def piece_order(d):
    return list(range(PIECES)) if d == 1 else list(range(PIECES))[::-1]


def ring_gather(ring, own_ref, all_ref, send_sem, recv_sem, psend, precv, on_hop):
    rows = own_ref.shape[0]
    size = rows // PIECES
    far = ring.nz // 2

    def piece(off, core, q):
        return all_ref.at[ring.chip(off), pl.ds(pl.multiple_of(core * rows + q * size, size), size)]

    def moves(d, k):
        return piece_order(d)[:PIECES // 2] if k == far - 1 else piece_order(d)

    def forward(d, k, q):
        dst = piece(-d * k, ring.c, q)
        src = own_ref.at[pl.ds(q * size, size)] if k == 0 else dst
        return remote(src, dst, send_sem.at[side(d), k, q], recv_sem.at[side(d), k, q], ring.next[d])

    def arrival(d, k, q):
        ref = piece(-d * (k + 1), ring.c, q)
        return remote(ref, ref, send_sem.at[side(d), k, q], recv_sem.at[side(d), k, q], ring.next[d])

    def pair(d, k, q, core):
        ref = piece(-d * (k + 1), core, q)
        return remote(ref, ref, psend.at[side(d), k, q], precv.at[side(d), k, q], ring.sib)

    def own_pair(core):
        ref = all_ref.at[ring.z, pl.ds(pl.multiple_of(core * rows, rows), rows)]
        return remote(own_ref, ref, psend.at[0, far, 0], precv.at[0, far, 0], ring.sib)

    for i in range(PIECES):
        for d in (1, -1):
            forward(d, 0, piece_order(d)[i]).start()
    own_pair(ring.c).start()
    all_ref[ring.z, pl.ds(pl.multiple_of(ring.c * rows, rows), rows)] = own_ref[...]
    own_pair(1 - ring.c).wait_recv()
    on_hop((0,))
    for k in range(far):
        for i in range(len(moves(1, k))):
            for d in (1, -1):
                q = moves(d, k)[i]
                arrival(d, k, q).wait_recv()
                if k + 1 < far and q in moves(d, k + 1):
                    forward(d, k + 1, q).start()
                pair(d, k, q, ring.c).start()
        for d in (1, -1):
            for q in moves(d, k):
                pair(d, k, q, 1 - ring.c).wait_recv()
        on_hop((k + 1, -(k + 1)) if k < far - 1 else (far,))

    def finish():
        for d in (1, -1):
            for k in range(far):
                for q in moves(d, k):
                    forward(d, k, q).wait_send()
                    pair(d, k, q, ring.c).wait_send()
        own_pair(ring.c).wait_send()

    return finish


def ring_scatter(ring, part_ref, give_ref, pair_ref, send_ref, recv_ref, send_sem, recv_sem, psend, precv, make, work):
    far = ring.nz // 2
    rows = give_ref.shape[1]
    size = rows // PIECES
    offs = [far]
    for k in range(far - 1, 0, -1):
        offs += [k, -k]
    offs.append(0)
    work = list(work)
    slots = {}
    for d in (1, -1):
        first = piece_order(d)[:PIECES // 2]
        rest = piece_order(d)[PIECES // 2:]
        if d == -1:
            rest = rest[::-1]
            rest = rest[::-1]
        slots[d] = [(far, q) for q in first]
        for k in range(far - 1, 0, -1):
            slots[d] += [(k, q) for q in rest + first]
    steps = len(slots[1])

    def pair(j):
        return remote(give_ref.at[j], pair_ref.at[j], psend.at[j], precv.at[j], ring.sib)

    def hop(d, s):
        i = side(d)
        return remote(send_ref.at[i, s], recv_ref.at[i, s], send_sem.at[i, s], recv_sem.at[i, s], ring.next[d])

    made = []

    def need(j):
        while len(made) <= j:
            i = len(made)
            part_ref[i] = make(offs[i])
            give_ref[i] = part_ref[i, pl.ds(pl.multiple_of((1 - ring.c) * rows, rows), rows)].astype(BF16)
            pair(i).start()
            made.append(i)

    paired = set()

    def base(j, q):
        if j not in paired:
            pair(j).wait_recv()
            paired.add(j)
        at = pl.multiple_of(ring.c * rows + q * size, size)
        return part_ref[j, pl.ds(at, size)] + pair_ref[j, pl.ds(q * size, size)].astype(F32)

    need(2)
    for s in range(steps):
        for d in (1, -1):
            k, q = slots[d][s]
            val = base(offs.index(d * k if k < far else far), q)
            if s >= PIECES:
                hop(d, s - PIECES).wait_recv()
                val = val + recv_ref[side(d), s - PIECES].astype(F32)
            send_ref[side(d), s] = val.astype(BF16)
            hop(d, s).start()
        if len(made) < len(offs):
            need(len(made))
        elif work:
            work.pop(0)()
    for w in work:
        w()

    def total(q):
        val = base(len(offs) - 1, q)
        for d in (1, -1):
            s = slots[d].index((1, q))
            hop(d, s).wait_recv()
            val = val + recv_ref[side(d), s].astype(F32)
        return val

    def finish():
        for d in (1, -1):
            for s in range(steps):
                hop(d, s).wait_send()
        for j in range(len(offs)):
            pair(j).wait_send()

    return total, finish


VM = pl.BlockSpec(memory_space=pltpu.VMEM)
ANY = pl.BlockSpec(memory_space=pl.ANY)


def comm_params(cid):
    return pltpu.CompilerParams(collective_id=cid, has_side_effects=True, vmem_limit_bytes=62 * 1024 * 1024)


def sum_small(vals, n):
    r, width = vals.shape
    cols = width // n
    pad = -r % 8
    blocks = jnp.pad(vals, ((0, pad), (0, 0))).reshape(r + pad, n, cols).transpose(1, 0, 2)

    def body(in_ref, out_ref, got_ref, s1, r1, s2, r2):
        me = lax.axis_index('tp')
        bar = pltpu.get_barrier_semaphore()
        peers = [lax.rem(me + j, n) for j in range(n)]
        for j in range(1, n):
            pl.semaphore_signal(bar, inc=1, device_id={'tp': peers[j]}, device_id_type=MESH)
        pl.semaphore_wait(bar, n - 1)
        first = [None] + [remote(in_ref.at[peers[j]], got_ref.at[j], s1.at[j], r1.at[j], peers[j]) for j in range(1, n)]
        for j in range(1, n):
            first[j].start()
        acc = in_ref[me]
        for j in range(1, n):
            first[j].wait_recv()
            acc = acc + got_ref[j]
        got_ref[0] = acc
        out_ref[me] = acc
        second = [None] + [remote(got_ref.at[0], out_ref.at[me], s2.at[j], r2.at[j], peers[j]) for j in range(1, n)]
        for j in range(1, n):
            second[j].start()
        for j in range(1, n):
            src = lax.rem(me + n - j, n)
            remote(got_ref.at[0], out_ref.at[src], s2.at[j], r2.at[j], peers[j]).wait_recv()
        for j in range(1, n):
            first[j].wait_send()
            second[j].wait_send()

    out = pl.pallas_call(
        body, out_shape=jax.ShapeDtypeStruct(blocks.shape, F32), in_specs=[VM], out_specs=VM,
        scratch_shapes=[pltpu.VMEM(blocks.shape, F32)] + [pltpu.SemaphoreType.DMA((n,))] * 4,
        compiler_params=comm_params(1), name='sum_small')(blocks)
    return out.transpose(1, 0, 2).reshape(r + pad, width)[:r]


class Local:
    def __init__(self, sems):
        self.sems = sems
        self.used = 0
        self.out = []

    def start(self, src, dst):
        copy = pltpu.make_async_copy(src, dst, self.sems.at[self.used])
        self.used += 1
        copy.start()
        return copy

    def save(self, src, dst):
        self.out.append(self.start(src, dst))

    def finish(self):
        for copy in self.out:
            copy.wait()


def phase(name, cid, n, rows, width, inputs, outputs, scratch, body):
    nz = n // 2
    far = nz // 2
    size = rows // PIECES
    steps = PIECES * (far - 1) + PIECES // 2
    comm = {
        'all': pltpu.VMEM((nz, 2 * rows, width), BF16), 'part': pltpu.VMEM((nz, 2 * rows, width), F32),
        'give': pltpu.VMEM((nz, rows, width), BF16), 'pair': pltpu.VMEM((nz, rows, width), BF16),
        'send': pltpu.VMEM((2, steps, size, width), BF16), 'recv': pltpu.VMEM((2, steps, size, width), BF16),
        'g0': pltpu.SemaphoreType.DMA((2, far + 1, PIECES)), 'g1': pltpu.SemaphoreType.DMA((2, far + 1, PIECES)),
        'g2': pltpu.SemaphoreType.DMA((2, far + 1, PIECES)), 'g3': pltpu.SemaphoreType.DMA((2, far + 1, PIECES)),
        's0': pltpu.SemaphoreType.DMA((2, steps)), 's1': pltpu.SemaphoreType.DMA((2, steps)),
        's2': pltpu.SemaphoreType.DMA((nz,)), 's3': pltpu.SemaphoreType.DMA((nz,)),
        'local': pltpu.SemaphoreType.DMA((16,)),
    }
    own = {key: pltpu.VMEM(*val) for key, val in scratch.items()}
    names = list(inputs) + list(outputs) + list(comm) + list(own)

    def kernel(*refs):
        r = types.SimpleNamespace(**dict(zip(names, refs)))
        ring = Ring(n)
        local = Local(r.local)

        def gather(on_hop):
            ring.enter()
            return ring_gather(ring, r.own, r.all, r.g0, r.g1, r.g2, r.g3, on_hop)

        def scatter(make, work=()):
            return ring_scatter(ring, r.part, r.give, r.pair, r.send, r.recv, r.s0, r.s1, r.s2, r.s3, make, work)

        body(r, ring, local, gather, scatter)
        local.finish()

    out = pl.pallas_call(
        kernel, out_shape=[jax.ShapeDtypeStruct(s, t) for s, t, _ in outputs.values()],
        in_specs=[spec for _, spec in inputs.values()], out_specs=[spec for _, _, spec in outputs.values()],
        scratch_shapes=list(comm.values()) + list(own.values()), compiler_params=comm_params(cid), name=name,
    )(*[arr for arr, _ in inputs.values()])
    return types.SimpleNamespace(**dict(zip(outputs, out)))


def dot(a, b, ca=1, cb=0):
    return lax.dot_general(a, b, (((ca,), (cb,)), ((), ())), preferred_element_type=F32)


def layer_norm(row_vals, ln_gain, ln_shift):
    mean_val = jnp.mean(row_vals, axis=-1, keepdims=True)
    centered = row_vals - mean_val
    var_val = jnp.mean(centered * centered, axis=-1, keepdims=True)
    return centered * lax.rsqrt(var_val + 1e-5) * ln_gain + ln_shift


def layer_norm_back(d_out, row_vals, ln_gain):
    mean_val = jnp.mean(row_vals, axis=-1, keepdims=True)
    centered = row_vals - mean_val
    var_val = jnp.mean(centered * centered, axis=-1, keepdims=True)
    inv = lax.rsqrt(var_val + 1e-5)
    unit = centered * inv
    scaled = d_out * ln_gain
    pull = scaled - jnp.mean(scaled, axis=-1, keepdims=True) - unit * jnp.mean(scaled * unit, axis=-1, keepdims=True)
    return pull * inv, d_out * unit


GELU_C = math.sqrt(2.0 / math.pi)


def gelu(x):
    return x * (0.5 * (1.0 + jnp.tanh(GELU_C * (x + 0.044715 * (x * x * x)))))


def gelu_slope(x):
    t = jnp.tanh(GELU_C * (x + 0.044715 * (x * x * x)))
    return 0.5 * (1.0 + t) + 0.5 * x * (1.0 - t * t) * (GELU_C * (1.0 + 3 * 0.044715 * (x * x)))


def rows_of(ref, ring, offs):
    parts = [ref[ring.chip(o)] for o in offs]
    return parts[0] if len(parts) == 1 else jnp.concatenate(parts, axis=0)


def put_rows(ref, ring, offs, vals):
    m = ref.shape[1]
    for i, o in enumerate(offs):
        ref[ring.chip(o)] = vals[i * m:(i + 1) * m].astype(ref.dtype)


def flat(ref, cols=None):
    vals = ref[...] if cols is None else ref[:, :, cols]
    return vals.reshape(vals.shape[0] * vals.shape[1], vals.shape[2])


def forward_tail(r, total, bias, next_ln):
    size = r.own.shape[0] // PIECES
    for q in range(PIECES):
        at = pl.ds(q * size, size)
        res = r.res[at] + total(q) + bias
        r.res_out[at] = res
        r.own_out[at] = (res if next_ln is None else layer_norm(res, next_ln[0], next_ln[1])).astype(BF16)


def attention_forward(n, l, own, res, ln_par, bias_d, wq, w_out):
    rows, width = own.shape
    nz, e = n // 2, wq.shape[-1]
    blk = (nz, 2 * rows)

    def body(r, ring, local, gather, scatter):
        got_q = [local.start(r.wq.at[l, i], r.wq_v.at[:, pl.ds(i * e, e)]) for i in range(3)]
        got_o = local.start(r.wo.at[l], r.wo_v)

        def on_hop(offs):
            if offs == (0,):
                for g in got_q:
                    g.wait()
            vals = dot(rows_of(r.all, ring, offs), r.wq_v[...]).astype(BF16)
            for i, ref in enumerate((r.q, r.k, r.v)):
                put_rows(ref, ring, offs, vals[:, i * e:(i + 1) * e])

        done = gather(on_hop)
        got_o.wait()
        local.save(r.all, r.h_all)
        seq = nz * 2 * rows

        def make(off):
            chip = ring.chip(off)
            s = dot(r.q[chip], flat(r.k), 1, 1) * e ** -0.5
            row = lax.broadcasted_iota(jnp.int32, s.shape, 0) + chip * (2 * rows)
            col = lax.broadcasted_iota(jnp.int32, s.shape, 1)
            s = jnp.where(row >= col, s, -1e30)
            s = jnp.exp(s - jnp.max(s, axis=-1, keepdims=True))
            p = (s / jnp.sum(s, axis=-1, keepdims=True)).astype(BF16)
            r.prob_v[chip] = p
            a = dot(p, flat(r.v)).astype(BF16)
            r.attn[chip] = a
            return dot(a, r.wo_v[...])

        total, finish = scatter(make, [lambda: local.save(r.prob_v, r.prob)])
        forward_tail(r, total, r.bias[l, 0:1], (r.ln[l, 2:3], r.ln[l, 3:4]))
        done()
        finish()

    return phase(
        f'attn_fwd_{l}', 2 + l, n, rows, width,
        dict(own=(own, VM), res=(res, VM), ln=(ln_par, VM), bias=(bias_d, VM), wq=(wq, ANY), wo=(w_out, ANY)),
        dict(h_all=(blk + (width,), BF16, ANY), q=(blk + (e,), BF16, VM), k=(blk + (e,), BF16, VM), v=(blk + (e,), BF16, VM),
             prob=(blk + (nz * 2 * rows,), BF16, ANY), attn=(blk + (e,), BF16, VM),
             res_out=((rows, width), F32, VM), own_out=((rows, width), BF16, VM)),
        dict(wq_v=((width, 3 * e), BF16), wo_v=((e, width), BF16), prob_v=(blk + (nz * 2 * rows,), BF16)), body)


def mlp_forward(n, l, own, res, ln_par, bias_d, w_up, b_up, w_down):
    rows, width = own.shape
    nz, f = n // 2, w_up.shape[-1]
    blk = (nz, 2 * rows)
    last = l + 1 == ln_par.shape[0]

    def body(r, ring, local, gather, scatter):
        got_u = local.start(r.wu.at[l], r.wu_v)
        got_d = local.start(r.wd.at[l], r.wd_v)

        def on_hop(offs):
            if offs == (0,):
                got_u.wait()
            pre = dot(rows_of(r.all, ring, offs), r.wu_v[...]) + r.bup[l:l + 1]
            put_rows(r.pre_v, ring, offs, pre)
            put_rows(r.act_v, ring, offs, gelu(pre))

        done = gather(on_hop)
        got_d.wait()
        local.save(r.all, r.h_all)
        local.save(r.pre_v, r.pre)
        local.save(r.act_v, r.act)
        total, finish = scatter(lambda off: dot(r.act_v[ring.chip(off)], r.wd_v[...]))
        forward_tail(r, total, r.bias[l, 1:2], None if last else (r.ln[l + 1, 0:1], r.ln[l + 1, 1:2]))
        done()
        finish()

    return phase(
        f'mlp_fwd_{l}', 4 + l, n, rows, width,
        dict(own=(own, VM), res=(res, VM), ln=(ln_par, VM), bias=(bias_d, VM), wu=(w_up, ANY), bup=(b_up, VM), wd=(w_down, ANY)),
        dict(h_all=(blk + (width,), BF16, ANY), pre=(blk + (f,), F32, ANY), act=(blk + (f,), BF16, ANY),
             res_out=((rows, width), F32, VM), own_out=((rows, width), BF16, VM)),
        dict(wu_v=((width, f), BF16), wd_v=((f, width), BF16), pre_v=(blk + (f,), F32), act_v=(blk + (f,), BF16)), body)


def backward_tail(r, total, gain):
    size = r.own.shape[0] // PIECES
    d_gain = d_shift = d_bias = 0.0
    for q in range(PIECES):
        at = pl.ds(q * size, size)
        d_h = total(q)
        d_in, gain_terms = layer_norm_back(d_h, r.res[at], gain)
        d_gain = d_gain + jnp.sum(gain_terms, axis=0, keepdims=True)
        d_shift = d_shift + jnp.sum(d_h, axis=0, keepdims=True)
        d_old = r.d_res[at]
        d_bias = d_bias + jnp.sum(d_old, axis=0, keepdims=True)
        d_new = d_old + d_in
        r.d_res_out[at] = d_new
        r.own_out[at] = d_new.astype(BF16)
    r.small[0:1] = d_gain
    r.small[1:2] = d_shift
    r.small[2:3] = d_bias


def mlp_backward(n, l, own, d_res, res, ln_par, h_all, pre, act, w_up, w_down):
    rows, width = own.shape
    nz, f = n // 2, w_up.shape[-1]
    blk = (nz, 2 * rows)

    def body(r, ring, local, gather, scatter):
        got_d = local.start(r.wd.at[l], r.wd_v)
        got_p = local.start(r.pre, r.pre_v)
        got_u = local.start(r.wu.at[l], r.wu_v)
        got_a = local.start(r.act, r.act_v)
        got_h = local.start(r.h_all, r.h_v)
        sums = []

        def on_hop(offs):
            if offs == (0,):
                got_d.wait()
                got_p.wait()
            d_act = dot(rows_of(r.all, ring, offs), r.wd_v[...], 1, 1)
            d_pre = d_act * gelu_slope(rows_of(r.pre_v, ring, offs))
            sums.append(jnp.sum(d_pre, axis=0, keepdims=True))
            put_rows(r.d_pre, ring, offs, d_pre)

        done = gather(on_hop)
        r.d_bup[...] = sum(sums)
        got_u.wait()
        got_a.wait()
        got_h.wait()
        step = 256

        def down_part(i):
            cols = pl.ds(i * step, step)
            r.dwd_v[:, cols] = dot(flat(r.act_v), flat(r.all, cols), 0, 0).astype(BF16)

        def up_part(i):
            cols = pl.ds(i * step, step)
            r.dwu_v[cols] = dot(flat(r.h_v, cols), flat(r.d_pre), 0, 0).astype(BF16)

        work = [lambda i=i, g=g: g(i) for i in range(width // step) for g in (down_part, up_part)]
        total, finish = scatter(lambda off: dot(r.d_pre[ring.chip(off)], r.wu_v[...], 1, 1), work)
        local.save(r.dwd_v, r.dwd)
        local.save(r.dwu_v, r.dwu)
        backward_tail(r, total, r.ln[l, 2:3])
        done()
        finish()

    return phase(
        f'mlp_bwd_{l}', 6 + l, n, rows, width,
        dict(own=(own, VM), d_res=(d_res, VM), res=(res, VM), ln=(ln_par, VM), h_all=(h_all, ANY), pre=(pre, ANY), act=(act, ANY),
             wu=(w_up, ANY), wd=(w_down, ANY)),
        dict(dwu=((width, f), BF16, ANY), dwd=((f, width), BF16, ANY), d_bup=((1, f), F32, VM), small=((8, width), F32, VM),
             d_res_out=((rows, width), F32, VM), own_out=((rows, width), BF16, VM)),
        dict(wu_v=((width, f), BF16), wd_v=((f, width), BF16), pre_v=(blk + (f,), F32), act_v=(blk + (f,), BF16),
             h_v=(blk + (width,), BF16), d_pre=(blk + (f,), BF16), dwu_v=((width, f), BF16), dwd_v=((f, width), BF16)), body)


def attention_backward(n, l, own, d_res, res, ln_par, saved, wq, w_out):
    rows, width = own.shape
    nz, e = n // 2, wq.shape[-1]
    blk = (nz, 2 * rows)
    seq = nz * 2 * rows

    def body(r, ring, local, gather, scatter):
        got_o = local.start(r.wo.at[l], r.wo_v)
        got_p = local.start(r.prob, r.prob_v)
        got_q = [local.start(r.wq.at[l, i], r.wq_v.at[:, pl.ds(i * e, e)]) for i in range(3)]
        got_h = local.start(r.h_all, r.h_v)
        r.d_k[...] = jnp.zeros_like(r.d_k)
        r.d_v[...] = jnp.zeros_like(r.d_v)

        def on_hop(offs):
            if offs == (0,):
                got_o.wait()
                got_p.wait()
            d_attn = dot(rows_of(r.all, ring, offs), r.wo_v[...], 1, 1).astype(BF16)
            prob = rows_of(r.prob_v, ring, offs)
            d_prob = dot(d_attn, flat(r.v), 1, 1)
            row_dot = jnp.sum(d_prob * prob, axis=-1, keepdims=True)
            d_score = (prob * (d_prob - row_dot) * e ** -0.5).astype(BF16)
            d_q = dot(d_score, flat(r.k)).astype(BF16)
            for i, o in enumerate(offs):
                r.d_proj[ring.chip(o), :, 0:e] = d_q[i * 2 * rows:(i + 1) * 2 * rows]
            r.d_k[...] += dot(d_score, rows_of(r.q, ring, offs), 0, 0)
            r.d_v[...] += dot(prob, d_attn, 0, 0)

        done = gather(on_hop)
        r.d_proj[:, :, e:2 * e] = r.d_k[...].astype(BF16).reshape(blk + (e,))
        r.d_proj[:, :, 2 * e:] = r.d_v[...].astype(BF16).reshape(blk + (e,))
        for g in got_q:
            g.wait()
        got_h.wait()
        step = 256

        def out_part(i):
            cols = pl.ds(i * step, step)
            r.dwo[:, cols] = dot(flat(r.attn), flat(r.all, cols), 0, 0).astype(BF16)

        def proj_part(i):
            cols = pl.ds(i * step, step)
            vals = dot(flat(r.h_v, cols), flat(r.d_proj), 0, 0).astype(BF16)
            for j in range(3):
                r.dwq[j, cols] = vals[:, j * e:(j + 1) * e]

        work = [lambda i=i, g=g: g(i) for i in range(width // step) for g in (out_part, proj_part)]
        total, finish = scatter(lambda off: dot(r.d_proj[ring.chip(off)], r.wq_v[...], 1, 1), work)
        backward_tail(r, total, r.ln[l, 0:1])
        done()
        finish()

    s = saved
    return phase(
        f'attn_bwd_{l}', 8 + l, n, rows, width,
        dict(own=(own, VM), d_res=(d_res, VM), res=(res, VM), ln=(ln_par, VM), h_all=(s.h_all, ANY), q=(s.q, VM), k=(s.k, VM), v=(s.v, VM),
             prob=(s.prob, ANY), attn=(s.attn, VM), wq=(wq, ANY), wo=(w_out, ANY)),
        dict(dwq=((3, width, e), BF16, VM), dwo=((e, width), BF16, VM), small=((8, width), F32, VM),
             d_res_out=((rows, width), F32, VM), own_out=((rows, width), BF16, VM)),
        dict(wq_v=((width, 3 * e), BF16), wo_v=((e, width), BF16), prob_v=(blk + (seq,), BF16), h_v=(blk + (width,), BF16),
             d_proj=(blk + (3 * e,), BF16), d_k=((seq, e), F32), d_v=((seq, e), F32)), body)


def solution(mesh):
    n = mesh.shape['tp']

    def device_step(x_loc, dy_loc, ln_par, bias_d, w_qkv, w_out, w_up, b_up, w_down):
        n_layers = ln_par.shape[0]
        res = x_loc[0].astype(F32)
        wq = jnp.transpose(w_qkv[:, :, :, 0], (0, 2, 1, 3))
        wo = w_out[:, 0]
        own = layer_norm(res, ln_par[0, 0], ln_par[0, 1]).astype(BF16)
        saved = []
        for l in range(n_layers):
            att = attention_forward(n, l, own, res, ln_par, bias_d, wq, wo)
            mlp = mlp_forward(n, l, att.own_out, att.res_out, ln_par, bias_d, w_up, b_up, w_down)
            saved.append((res, att, mlp))
            own, res = mlp.own_out, mlp.res_out
        y_loc = own

        own, d_res = dy_loc[0], dy_loc[0].astype(F32)
        grads = [None] * n_layers
        for l in reversed(range(n_layers)):
            res_one, att, mlp = saved[l]
            b_mlp = mlp_backward(n, l, own, d_res, att.res_out, ln_par, mlp.h_all, mlp.pre, mlp.act, w_up, w_down)
            b_att = attention_backward(n, l, b_mlp.own_out, b_mlp.d_res_out, res_one, ln_par, att, wq, wo)
            own, d_res = b_att.own_out, b_att.d_res_out
            small = jnp.concatenate([b_att.small[:2], b_mlp.small[:2], b_att.small[2:3], b_mlp.small[2:3]])
            grads[l] = (small, b_att.dwq, b_att.dwo, b_mlp.dwu, b_mlp.d_bup[0], b_mlp.dwd)
        small = sum_small(jnp.concatenate([g[0] for g in grads], axis=0), n)
        small = small.reshape(n_layers, 6, small.shape[-1])
        stacked = [jnp.stack([g[i] for g in grads]) for i in range(1, 6)]
        return (y_loc[None], own[None], small[:, :4], small[:, 4:],
                jnp.transpose(stacked[0], (0, 2, 1, 3))[:, :, :, None], stacked[1][:, None],
                stacked[2], stacked[3], stacked[4])

    in_specs = (P('dp', 'tp', None), P('dp', 'tp', None), P(None, None, None), P(None, None, None),
                P(None, None, None, 'tp', None), P(None, 'tp', None, None), P(None, None, 'tp'), P(None, 'tp'), P(None, 'tp', None))
    out_specs = (P('dp', 'tp', None), P('dp', 'tp', None), P('dp', None, None), P('dp', None, None),
                 P('dp', None, None, 'tp', None), P('dp', 'tp', None, None), P('dp', None, 'tp'), P('dp', 'tp'), P('dp', 'tp', None))
    return jax.shard_map(device_step, mesh=mesh, in_specs=in_specs, out_specs=out_specs, check_vma=False)
```

time: 692 us -> 514 us (0.74)
  matrix products: 117 us -> 0 us
  Pallas kernels: 506 us -> 470 us
  other arithmetic: 40 us -> 20.4 us
    dot_general x46 -> x0, matrix products: 117 us -> none  [mm(): return jnp.einsum(spec, a, b, preferred_element_type=F32)]
    pallas_call x16 -> x8, Pallas kernels: 476 us -> 452 us  [phase(): pl.pallas_call(kernel, out_shape=[jax.ShapeDtypeStruct(s, t) for s, t, _...]
    reduce_sum x12 -> x0, other arithmetic: 14.2 us -> none  [the longest x5 7 us: layer_norm(): return centered * lax.rsqrt(var_val + 1e-05) * ln_gain + ln_shift]
    unnamed x2 -> x0, Pallas kernels: 9.23 us -> none
    unnamed x102 -> x18, local copies, waits for them, and re-layouts: 10.5 us -> 1.44 us
where the time goes in v2:
time: 514 us; the launch traced here: 504 us
  Pallas kernels  470 us (91%)
  other arithmetic  20.4 us (4%)
  local copies, waits for them, and re-layouts  12.2 us (2%)
    pallas_call x8, Pallas kernels, phase(): pl.pallas_call(kernel, out_shape=[jax.ShapeDtypeStruct(s, t) for s, t, _...  452 us
    pallas_call x1, Pallas kernels, sum_small(): pl.pallas_call(body, out_shape=jax.ShapeDtypeStruct(blocks.shape, F32), i...  19 us

profile of v2, /device:TPU:21, one launch (start us, length us, event | category | flops | bytes accessed | tf_op | source)
XLA Modules:
  0.0 504.1 jit_solution(13169410322046369862)
XLA Ops:
  0.6 1.1 convert_reduce_fusion
  1.7 1.2 multiply_reduce_fusion
  3.0 0.9 fusion
  3.8 1.8 add_convert_fusion.refs_0_
  5.6 1.8 convert_bitcast_fusion.refs_1_.refs_2_
  7.4 1.8 bitcast_convert_fusion.refs_1_
  9.2 61.5 %attn_fwd_0.1 = (bf16[8,128,2048]{2,1,0:T(8,128)(2,1)}, bf16[8,128,128]{2,1,0:T(8,128)(2,1)}, bf16[8,128,128]{2,1,0:T(8,128)(2,1)}, bf16[8,128,128]{2,1,0:T(8,12...) custom-call(bf16[64,2048]{1,0:T(8,128)(2,1)} %add_convert_fusion.ref, ...), custom_call_target="tpu_custom_call" | custom-call | tf_op jit(solution)/shard_map/attn_fwd_0/pallas_call | solution.py:293
  70.7 54.0 %mlp_fwd_0.1 = (bf16[8,128,2048]{2,1,0:T(8,128)(2,1)}, f32[8,128,512]{2,1,0:T(8,128)}, bf16[8,128,512]{2,1,0:T(8,128)(2,1)}, f32[64,2048]{1,0:T(8,128)}, bf16[64,2048]{1,0:T(8,128)(2,1)}) custom-call(bf16[64,2048]{1,0:T(8,128)(2,1)} %get-tuple-element.55.refs_0_, f32[64,2048]{1,0:T(8,128)} %get-tuple-element.56.refs_1_.refs_2_, f32[2,4,2048]{2,1,0:T(4,128)} %refs_3_.15, ...), custom_call_target="tpu_custom_call" | custom-call | tf_op jit(solution)/shard_map/mlp_fwd_0/pallas_call | solution.py:293
  124.7 55.7 %attn_fwd_1.1 = (bf16[8,128,2048]{2,1,0:T(8,128)(2,1)}, bf16[8,128,128]{2,1,0:T(8,128)(2,1)}, bf16[8,128,128]{2,1,0:T(8,128)(2,1)}, bf16[8,128,128]{2,1,0:T(8,12...) custom-call(bf16[64,2048]{1,0:T(8,128)(2,1)} %get-tuple-element.57.r, ...), custom_call_target="tpu_custom_call" | custom-call | tf_op jit(solution)/shard_map/attn_fwd_1/pallas_call | solution.py:293
  180.5 53.4 %mlp_fwd_1.1 = (bf16[8,128,2048]{2,1,0:T(8,128)(2,1)}, f32[8,128,512]{2,1,0:T(8,128)}, bf16[8,128,512]{2,1,0:T(8,128)(2,1)}, f32[64,2048]{1,0:T(8,128)}, bf16[64,2048]{1,0:T(8,128)(2,1)}) custom-call(bf16[64,2048]{1,0:T(8,128)(2,1)} %get-tuple-element.59.refs_0_, f32[64,2048]{1,0:T(8,128)} %get-tuple-element.60.refs_1_.refs_2_, f32[2,4,2048]{2,1,0:T(4,128)} %refs_3_.15, ...), custom_call_target="tpu_custom_call" | custom-call | tf_op jit(solution)/shard_map/mlp_fwd_1/pallas_call | solution.py:293
  233.9 56.1 %mlp_bwd_1.1 = (bf16[2048,512]{1,0:T(8,128)(2,1)}, bf16[512,2048]{1,0:T(8,128)(2,1)}, f32[1,512]{1,0:T(1,128)}, f32[8,2048]{1,0:T(8,128)}, f32[64,2048]{1,0:T(8,128)}, /*index=5*/bf16[64,2048]{1,0:T(8,128)(2,1)}) custom-call(bf16[64,2048]{1,0:T(8,128)(2,1)} %bitcast.57, f32[64,2048]{1,0:T(8,128)} %bitcast_convert_fusion.refs_1_, ...), custom_call_target="tpu_custom_call" | custom-call | tf_op jit(solution)/shard_map/mlp_bwd_1/pallas_call | solution.py:293
  290.0 57.3 %attn_bwd_1.1 = (bf16[3,2048,128]{2,1,0:T(8,128)(2,1)}, bf16[128,2048]{1,0:T(8,128)(2,1)}, f32[8,2048]{1,0:T(8,128)}, f32[64,2048]{1,0:T(8,128)}, bf16[64,2048]{1,0:T(8,128)(2,1)}) custom-call(bf16[64,2048]{1,0:T(8,128)(2,1)} %get-tuple-element.65.refs_0_, f32[64,2048]{1,0:T(8,128)} %get-tuple-element.66.refs_1_, ...), custom_call_target="tpu_custom_call" | custom-call | tf_op jit(solution)/shard_map/attn_bwd_1/pallas_call | solution.py:293
  347.3 56.1 %mlp_bwd_0.1 = (bf16[2048,512]{1,0:T(8,128)(2,1)}, bf16[512,2048]{1,0:T(8,128)(2,1)}, f32[1,512]{1,0:T(1,128)}, f32[8,2048]{1,0:T(8,128)}, f32[64,2048]{1,0:T(8,128)}, /*index=5*/bf16[64,2048]{1,0:T(8,128)(2,1)}) custom-call(bf16[64,2048]{1,0:T(8,128)(2,1)} %get-tuple-element.73.refs_0_, f32[64,2048]{1,0:T(8,128)} %get-tuple-element.74.refs_1_, ...), custom_call_target="tpu_custom_call" | custom-call | tf_op jit(solution)/shard_map/mlp_bwd_0/pallas_call | solution.py:293
  403.4 0.0 copy-start.3
  403.4 57.4 %attn_bwd_0.1 = (bf16[3,2048,128]{2,1,0:T(8,128)(2,1)}, bf16[128,2048]{1,0:T(8,128)(2,1)}, f32[8,2048]{1,0:T(8,128)}, f32[64,2048]{1,0:T(8,128)}, bf16[64,2048]{1,0:T(8,128)(2,1)}) custom-call(bf16[64,2048]{1,0:T(8,128)(2,1)} %get-tuple-element.78.refs_0_, f32[64,2048]{1,0:T(8,128)} %get-tuple-element.79.refs_1_, ...), custom_call_target="tpu_custom_call" | custom-call | tf_op jit(solution)/shard_map/attn_bwd_0/pallas_call | solution.py:293
  460.8 0.0 copy-done.3
  460.8 0.0 copy-start.6
  460.8 0.0 copy-start.7
  460.8 3.4 maximum_bitcast_fusion
  464.2 0.0 copy-done.6
  464.2 0.0 copy-done.7
  464.2 0.6 pad_maximum_fusion.2
  464.8 0.8 slice.44
  465.6 0.8 slice.42
  466.5 0.8 slice.45
  467.3 0.8 slice.43
  468.2 0.8 slice.48
  469.0 0.8 slice.46
  469.9 0.8 slice.49
  470.7 0.8 slice.47
  471.6 0.1 concatenate.3
  471.7 0.7 bitcast_bitcast_fusion.in_ref
  472.3 19.0 %sum_small.1 = f32[16,16,128]{2,1,0:T(8,128)} custom-call(f32[16,16,128]{2,1,0:T(8,128)} %bitcast_bitcast_fusion.in_ref), custom_call_target="tpu_custom_call" | custom-call | tf_op jit(solution)/shard_map/sum_small/pallas_call | solution.py:233
  491.3 0.0 copy-start.1
  491.3 1.1 copy.21
  492.4 0.6 slice.55
  493.1 0.6 slice.54
  493.7 2.3 maximum_bitcast_fusion.1
  496.0 0.0 copy-done.1
  496.0 0.0 copy-start
  496.0 0.0 copy-start.2
  496.0 4.1 pad_maximum_fusion
  500.1 0.0 copy-done
  500.1 0.0 copy-done.2
  500.1 0.0 copy-start.4
  500.1 0.0 copy-start.5
  500.1 2.4 pad_maximum_fusion.1
  502.5 0.0 copy-done.4
  502.5 0.7 copy.28
  503.2 0.0 copy-done.5
  503.2 0.7 copy.29
  (3 shorter events, 0.0 us)
Async XLA Ops:
  403.4 57.4 %copy-start.3 = (bf16[3,2048,128]{2,1,0:T(8,128)(2,1)S(1)}, bf16[3,2048,128]{2,1,0:T(8,128)(2,1)}, u32[]{:S(2)}) copy-start(bf16[3,2048,128]{2,1,0:T(8,128)(2,1)} %get-tuple-element.92) | copy-start | bytes 4718596
  460.8 3.4 copy-start.6
  460.8 3.4 copy-start.7
  491.3 4.7 copy-start.1
  496.0 4.1 copy-start
  496.0 4.1 copy-start.2
  500.1 2.4 copy-start.4
  500.1 3.1 copy-start.5
